TPU v7x, 256 devices: a whole 4x4x8 slice. The times are simulated.
256 devices in a mesh: blk: 32 (over x, z_hi, core), grp: 8 (over y, z_lo).
Axes of the slice: x: 4, y: 4, z: 8 (z_hi: 4, z_lo: 2; z = z_hi * 2 + z_lo), core: 2. Of those that a mesh axis runs over, the one named last changes fastest.
Arguments:
- residents: bfloat16 [512, 32, 1024], P(('blk', 'grp')), may hold values from -6 to 6
- travellers: bfloat16 [64, 32, 1024], P('blk'), may hold values from -6 to 6
- pair_list: int32 [256, 4, 2, 3], P(('blk', 'grp')), may hold values from 0 to 1, as said below
Outputs:
- resident_exchange: float32 [512, 32, 1024], P(('blk', 'grp'))
- traveller_exchange: float32 [64, 32, 1024], P('blk', 'grp')
Inputs may be any that keep to these rules, and one draw needn't show every extreme that they name: `pair_list`: entry 0 is a resident index below 2, entry 1 a traveller index below 2, entry 2 is 0 or 1; the number of active slots differs from device to device.
All inputs are finite; a program needn't handle non-finite values.
Results may differ from a plain program's by a relative error of at most 0.0003.
Values may be sent and summed in bfloat16 or wider, within the bound.
A program may use at most 64 MiB of HBM per device.

v0:
```python
import functools

import jax
import jax.numpy as jnp
import numpy as np
from jax import lax
from jax.experimental import pallas as pl
from jax.experimental.pallas import tpu as pltpu
from jax.sharding import PartitionSpec as P

MESH = pl.DeviceIdType.MESH
F32, BF16, I16 = jnp.float32, jnp.bfloat16, jnp.int16
TOP = 32767.0


def tables(edge):
    half = edge // 2
    index = np.arange(edge, dtype=np.float64) + 1.0
    sine = np.sqrt(2.0 / (edge + 1)) * np.sin(np.pi * np.outer(index, index) / (edge + 1))
    eigen = 2.0 - 2.0 * np.cos(np.pi * index / (edge + 1))
    perm = np.zeros((2, 256, 256))
    for b8 in range(8):
        for c in range(edge):
            rc, cc = (0, c) if c < half else (1, edge - 1 - c)
            perm[0, b8 * edge + c, rc * 128 + b8 * half + cc] = 1.0
            perm[1, b8 * edge + c, rc * 128 + (7 - b8) * half + cc] = 1.0
    perms = np.concatenate([perm, perm.transpose(0, 2, 1)])
    planes, scales = [], []
    for pb in range(2):
        for pc in range(2):
            planes.append(np.kron(sine[pb::2, :half].T, sine[pc::2, :half].T))
            scales.append(
                1.0
                / (
                    eigen[:, None, None]
                    + eigen[None, pb::2, None]
                    + eigen[None, None, pc::2]
                ).reshape(edge, half * half)
            )
    planes = np.stack(planes)
    both = np.stack([planes, planes.transpose(0, 2, 1)]).astype(np.float32)
    high = both.astype(jnp.bfloat16)
    low = (both - high.astype(np.float32)).astype(jnp.bfloat16)
    weights = np.stack([high, low], axis=2)
    small = np.kron(np.eye(2), sine).astype(np.float32)
    small_high = small.astype(jnp.bfloat16)
    small_low = (small - small_high.astype(np.float32)).astype(jnp.bfloat16)
    rows = np.concatenate([small_high, small_high, small_low, small_low], axis=1)
    return (
        perms.astype(jnp.bfloat16),
        weights,
        rows,
        np.stack(scales).astype(np.float32),
    )


def dot(a, b):
    return jnp.dot(a, b, preferred_element_type=F32)


def split(x):
    high = x.astype(BF16)
    return high, (x - high.astype(F32)).astype(BF16)


def permuted(x, perm_ref):
    halves = []
    for rb in range(2):
        parts = [[None, None], [None, None]]
        for n in range(2):
            m = n if rb == 0 else 3 - n
            y = dot(x[:, m * 256 : (m + 1) * 256], perm_ref[rb])
            parts[0][n], parts[1][n] = y[:, :128], y[:, 128:]
        halves.append(jnp.concatenate(parts[0] + parts[1], axis=1))
    return halves


def restored(halves, perm_ref):
    rows = halves[0].shape[0]
    groups = [None] * 4
    for rb in range(2):
        for n in range(2):
            m = n if rb == 0 else 3 - n
            x = jnp.concatenate(
                [
                    halves[rb][:, n * 128 : (n + 1) * 128],
                    halves[rb][:, 256 + n * 128 : 256 + (n + 1) * 128],
                ],
                axis=1,
            )
            y = dot(jnp.concatenate(split(x), axis=0), perm_ref[2 + rb])
            groups[m] = y[:rows] + y[rows:]
    return jnp.concatenate(groups, axis=1)


def plane(g, weight_ref, way):
    out = []
    for p in range(4):
        high, low = split(g[p])
        rows = high.shape[0]
        a = dot(jnp.concatenate([high, low], axis=0), weight_ref[way, p, 0])
        out.append(a[:rows] + a[rows:] + dot(high, weight_ref[way, p, 1]))
    return out


def along_rows(g, rows):
    out = []
    for p in range(4):
        high, low = split(g[p])
        out.append(dot(rows, jnp.concatenate([high, low, high, low], axis=0)))
    return out


def peak(tiles):
    tiles = [jnp.abs(t) for t in tiles]
    while len(tiles) > 1:
        tiles = [
            jnp.maximum(tiles[i], tiles[i + 1]) if i + 1 < len(tiles) else tiles[i]
            for i in range(0, len(tiles), 2)
        ]
    return jnp.maximum(tiles[0], 1e-30)


def lane_tiles(x):
    return [x[:, j * 128 : (j + 1) * 128] for j in range(x.shape[1] // 128)]


def coded(x, wide):
    return jnp.round(x * wide).astype(jnp.int32)


def spread(tile, times):
    return jnp.concatenate([tile] * times, axis=1)


def kernel(
    res_hbm,
    trav_hbm,
    pair_ref,
    perm_hbm,
    weight_hbm,
    rows_hbm,
    scale_hbm,
    res_out,
    trav_out,
    res_in,
    trav_in,
    perm_ref,
    weight_ref,
    rows_ref,
    scale_ref,
    load_sem,
    mine,
    tbuf,
    ubuf,
    res_acc,
    ycode,
    yscale,
    yown,
    yget,
    ygets,
    hcode,
    hscale,
    hget,
    hgets,
    z_send,
    d_send,
    f_send,
    t_recv,
    y_send,
    ys_send,
    y_recv,
    ys_recv,
    h_send,
    hs_send,
    h_recv,
    hs_recv,
):
    n_blk = lax.axis_size("blk")
    blk, grp = lax.axis_index("blk"), lax.axis_index("grp")
    core = lax.rem(blk, 2)
    y, lo = grp // 2, lax.rem(grp, 2)

    def around(b):
        return lax.rem(b + n_blk, n_blk)

    loads = [
        pltpu.make_async_copy(src, dst, load_sem.at[j])
        for j, (src, dst) in enumerate(
            (
                (trav_hbm, trav_in),
                (perm_hbm, perm_ref),
                (res_hbm, res_in),
                (rows_hbm, rows_ref),
                (scale_hbm, scale_ref),
                (weight_hbm, weight_ref),
            )
        )
    ]
    for load in loads:
        load.start()

    barrier = pltpu.get_barrier_semaphore()
    count = 0
    for d in range(1, 4):
        for other in range(2):
            to = (blk - core + other, lax.rem(y + d, 4) * 2 + lo)
            pl.semaphore_signal(barrier, inc=1, device_id=to, device_id_type=MESH)
            count += 1
    for s in (-4, -3, -2, -1, 1, 2, 3, 4):
        for z in range(2):
            to = (around(blk + s), y * 2 + z)
            pl.semaphore_signal(barrier, inc=1, device_id=to, device_id_type=MESH)
            count += 1

    loads[0].wait()
    loads[1].wait()
    own = [h.reshape(2, 4, 8, 512) for h in permuted(trav_in[...].reshape(64, 1024), perm_ref)]
    for q in range(4):
        for t in range(2):
            mine[q, t] = jnp.concatenate([own[0][t, q], own[1][t, q]], axis=0).astype(BF16)

    pl.semaphore_wait(barrier, count)

    def remote(src, dst, send, recv, to):
        return pltpu.make_async_remote_copy(
            src_ref=src, dst_ref=dst, send_sem=send, recv_sem=recv, device_id=to, device_id_type=MESH
        )

    hops = []
    for near in range(2):
        slot = near * 2 + core
        hop = remote(
            mine.at[y],
            tbuf.at[slot, y],
            z_send.at[near],
            t_recv.at[slot, y],
            (around(blk + (2 if near else 4)), y * 2 + 1 - lo),
        )
        hop.start()
        hops.append(hop)

    def across(q):
        return remote(mine.at[q], tbuf.at[0, q], d_send.at[q], t_recv.at[0, q], (blk - core + 1, grp))

    @pl.when(core == 0)
    def _():
        for q in range(4):
            across(q).start()

    loads[2].wait()
    for rb, h in enumerate(permuted(res_in[...].reshape(64, 1024), perm_ref)):
        for r in range(2):
            ubuf[r, rb] = h[r * 32 : (r + 1) * 32]
    res_acc[...] = jnp.zeros_like(res_acc)

    def forward(near, d, swap):
        slot = near * 2 + core
        to_core = 1 - core if swap else core
        return remote(
            tbuf.at[slot, y],
            tbuf.at[slot, y],
            f_send.at[near, d, int(swap)],
            t_recv.at[slot, y],
            (blk - core + to_core, lax.rem(y + d, 4) * 2 + lo),
        )

    for near in range(2):
        hops[near].wait_recv()
        for d in range(1, 4):
            forward(near, d, False).start()
        if near:
            for d in range(4):
                forward(near, d, True).start()
        else:

            @pl.when(core == 1)
            def _():
                for d in range(4):
                    forward(0, d, True).start()

    for load in loads[3:]:
        load.wait()

    def arrived(slot, q):
        remote(tbuf.at[slot, q], tbuf.at[slot, q], z_send.at[0], t_recv.at[slot, q], (blk, grp)).wait_recv()

    def y_copies(i, d):
        to = (blk, lax.rem(y + d, 4) * 2 + lo)
        q = lax.rem(y + d, 4)
        return (
            remote(ycode.at[i, q], yget.at[i, d - 1], y_send.at[i, d - 1], y_recv.at[i, d - 1], to),
            remote(yscale.at[i], ygets.at[i, d - 1], ys_send.at[i, d - 1], ys_recv.at[i, d - 1], to),
        )

    def h_copies(i, z):
        s = lax.rem(3 - i + core, 4)
        to = (around(blk - 1 - s), y * 2 + z)
        at = s * 2 + lo
        return (
            remote(hcode.at[i, z], hget.at[at], h_send.at[i, z], h_recv.at[at], to),
            remote(hscale.at[i], hgets.at[at], hs_send.at[i, z], hs_recv.at[at], to),
        )

    def solve(i):
        s = lax.rem(3 - i + core, 4)
        pick = [[pair_ref[0, s, p, e] for e in range(3)] for p in range(2)]
        both = []
        for t in range(2):
            wide = tbuf[i, :, t].astype(F32).reshape(4, 2, 8, 512)
            both.append([wide[:, rb].reshape(32, 512) for rb in range(2)])
        u, w = [], []
        for p in range(2):
            u.append([ubuf[pick[p][0], rb] for rb in range(2)])
            second = pick[p][1] == 1
            w.append([jnp.where(second, both[1][rb], both[0][rb]) for rb in range(2)])
        d = [jnp.concatenate([u[p][rb] * w[p][rb] for p in range(2)], axis=0) for rb in range(2)]
        g = []
        for e in (d[0] + d[1], d[0] - d[1]):
            g += [e[:, :256] + e[:, 256:], e[:, :256] - e[:, 256:]]
        rows = rows_ref[...]
        g = along_rows(plane(g, weight_ref, 0), rows)
        g = [
            (m.reshape(2, 32, 256) * scale_ref[p][None]).reshape(64, 256)
            for p, m in enumerate(g)
        ]
        g = plane(along_rows(g, rows), weight_ref, 1)
        pot = []
        for e, o in (
            (g[0] + g[2], g[1] + g[3]),
            (g[0] - g[2], g[1] - g[3]),
        ):
            pot.append(jnp.concatenate([e + o, e - o], axis=1))

        def factor(p, e, value):
            return jnp.where(pick[p][e] == value, pick[p][2], 0).astype(F32)

        terms = [[None, None], [None, None]]
        for rb in range(2):
            v = [pot[rb][p * 32 : (p + 1) * 32] for p in range(2)]
            vw = [v[p] * w[p][rb] for p in range(2)]
            vu = [v[p] * u[p][rb] for p in range(2)]
            for j in range(2):
                res_acc[j, rb] += vw[0] * factor(0, 0, j) + vw[1] * factor(1, 0, j)
                terms[j][rb] = vu[0] * factor(0, 1, j) + vu[1] * factor(1, 1, j)
        top = peak([t for j in range(2) for rb in range(2) for a in range(4) for t in lane_tiles(terms[j][rb][a * 8 : (a + 1) * 8])])
        yscale[i] = top * (1.0 / TOP)
        wide = spread(TOP / top, 4)[None]
        for j in range(2):
            parts = []
            for rb in range(2):
                t = terms[j][rb].reshape(4, 8, 512)
                parts.append(coded(t, wide))
                for q in range(4):
                    yown[i, q, j, rb] = t[q]
            for q in range(4):
                ycode[i, q, j] = jnp.concatenate([parts[0][q], parts[1][q]], axis=0).astype(I16)

    def gather(i):
        sums = [[yown[i, y, j, rb] for rb in range(2)] for j in range(2)]
        for d in range(1, 4):
            for copy in y_copies(i, d):
                copy.wait_recv()
            scale = spread(ygets[i, d - 1], 4)
            for j in range(2):
                code = yget[i, d - 1, j].astype(jnp.int32).astype(F32)
                for rb in range(2):
                    sums[j][rb] += code[rb * 8 : (rb + 1) * 8] * scale
        first = lax.broadcasted_iota(jnp.int32, (8, 512), 0) < 4
        out = [
            [jnp.where(first, sums[0][rb], pltpu.roll(sums[1][rb], 4, 0)) for rb in range(2)],
            [jnp.where(first, pltpu.roll(sums[0][rb], 4, 0), sums[1][rb]) for rb in range(2)],
        ]
        top = peak([t for z in range(2) for rb in range(2) for t in lane_tiles(out[z][rb])])
        hscale[i] = top * (1.0 / TOP)
        wide = spread(TOP / top, 4)
        for z in range(2):
            hcode[i, z] = jnp.concatenate([coded(out[z][rb], wide) for rb in range(2)], axis=0).astype(I16)
            for copy in h_copies(i, z):
                copy.start()

    def step(i, carry):
        for d in range(1, 4):
            arrived(i, lax.rem(y + d, 4))

        @pl.when(lax.rem(i, 2) != core)
        def _():
            arrived(i, y)

        solve(i)
        for d in range(1, 4):
            for copy in y_copies(i, d):
                copy.start()

        @pl.when(i > 0)
        def _():
            gather(i - 1)

        return carry

    lax.fori_loop(0, 4, step, 0)

    for r in range(2):
        res_out[r] = restored([res_acc[r, rb] for rb in range(2)], perm_ref)
    gather(3)

    total = [jnp.zeros((8, 512), F32) for _ in range(2)]
    for at in range(8):
        remote(hcode.at[0, 0], hget.at[at], h_send.at[0, 0], h_recv.at[at], (blk, grp)).wait_recv()
        remote(hscale.at[0], hgets.at[at], hs_send.at[0, 0], hs_recv.at[at], (blk, grp)).wait_recv()
        code = hget[at].astype(jnp.int32).astype(F32)
        scale = spread(hgets[at], 4)
        for rb in range(2):
            total[rb] += code[rb * 8 : (rb + 1) * 8] * scale
    trav_out[...] = restored(total, perm_ref).reshape(2, 4, 1024)

    for near in range(2):
        hops[near].wait_send()
        for d in range(1, 4):
            forward(near, d, False).wait_send()
    for d in range(4):
        forward(1, d, True).wait_send()

    @pl.when(core == 1)
    def _():
        for d in range(4):
            forward(0, d, True).wait_send()

    @pl.when(core == 0)
    def _():
        for q in range(4):
            across(q).wait_send()

    for i in range(4):
        for d in range(1, 4):
            for copy in y_copies(i, d):
                copy.wait_send()
        for z in range(2):
            for copy in h_copies(i, z):
                copy.wait_send()


def local(residents, travellers, pair_list):
    consts = tables(32)
    hbm = pl.BlockSpec(memory_space=pltpu.HBM)
    vmem = pl.BlockSpec(memory_space=pltpu.VMEM)
    dma = pltpu.SemaphoreType.DMA
    return pl.pallas_call(
        kernel,
        out_shape=(
            jax.ShapeDtypeStruct((2, 32, 1024), F32),
            jax.ShapeDtypeStruct((2, 4, 1024), F32),
        ),
        in_specs=[hbm, hbm, pl.BlockSpec(memory_space=pltpu.SMEM), hbm, hbm, hbm, hbm],
        out_specs=(vmem, vmem),
        scratch_shapes=[
            pltpu.VMEM((2, 32, 1024), BF16),
            pltpu.VMEM((2, 32, 1024), BF16),
            pltpu.VMEM((4, 256, 256), BF16),
            pltpu.VMEM((2, 4, 2, 256, 256), BF16),
            pltpu.VMEM((64, 256), BF16),
            pltpu.VMEM((4, 32, 256), F32),
            dma((6,)),
            pltpu.VMEM((4, 2, 16, 512), BF16),
            pltpu.VMEM((4, 4, 2, 16, 512), BF16),
            pltpu.VMEM((2, 2, 32, 512), F32),
            pltpu.VMEM((2, 2, 32, 512), F32),
            pltpu.VMEM((4, 4, 2, 16, 512), I16),
            pltpu.VMEM((4, 8, 128), F32),
            pltpu.VMEM((4, 4, 2, 2, 8, 512), F32),
            pltpu.VMEM((4, 3, 2, 16, 512), I16),
            pltpu.VMEM((4, 3, 8, 128), F32),
            pltpu.VMEM((4, 2, 16, 512), I16),
            pltpu.VMEM((4, 8, 128), F32),
            pltpu.VMEM((8, 16, 512), I16),
            pltpu.VMEM((8, 8, 128), F32),
            dma((2,)),
            dma((4,)),
            dma((2, 4, 2)),
            dma((4, 4)),
            dma((4, 3)),
            dma((4, 3)),
            dma((4, 3)),
            dma((4, 3)),
            dma((4, 2)),
            dma((4, 2)),
            dma((8,)),
            dma((8,)),
        ],
        compiler_params=pltpu.CompilerParams(collective_id=0, has_side_effects=True),
    )(residents, travellers, pair_list, *[jnp.asarray(c) for c in consts])


def solution(mesh):
    return jax.shard_map(
        local,
        mesh=mesh,
        in_specs=(
            P(("blk", "grp"), None, None),
            P("blk", None, None),
            P(("blk", "grp"), None, None, None),
        ),
        out_specs=(P(("blk", "grp"), None, None), P("blk", "grp", None)),
        check_vma=False,
    )
```

profile of v0, /device:TPU:1, one launch (start us, length us, event | category | flops | bytes accessed | tf_op | source)
XLA Modules:
  0.0 43.6 jit_solution(17627409001332906192)
XLA Ops:
  0.6 1.4 %copy.9.pair_ref = s32[1,4,2,3]{3,2,1,0:T(2,128)} copy(s32[1,4,2,3]{1,2,3,0:T(2,128)} %param.9) | data formatting | bytes 192 | tf_op args[2]
  2.0 38.6 %shard_map.86 = (f32[2,32,1024]{2,1,0:T(8,128)}, f32[2,4,1024]{2,1,0:T(4,128)}) custom-call(bf16[2,32,1024]{2,1,0:T(8,128)(2,1)} %res_hbm.1, bf16[2,32,1024]{2,1,0:T(8,128)(2,1)} %trav_hbm.1, s32[1,4,2,3]{3,2,1,0:T(2,128)} %copy.9.pair_ref, bf16[4,256,256]{2,1,0:T(8,128)(2,1)} %constant.8.clone.perm_hbm, ...), custom_call_target="tpu_custom_call" | custom-call | tf_op jit(solution)/shard_map/pallas_call | solution.py:448
  40.6 1.7 %copy.12 = f32[2,32,1024]{2,1,0:T(8,128)} copy(f32[2,32,1024]{2,1,0:T(8,128)} %get-tuple-element.4) | data formatting | bytes 524288
  42.2 1.4 %copy.13 = f32[2,4,1024]{2,1,0:T(4,128)} copy(f32[2,4,1024]{2,1,0:T(4,128)} %get-tuple-element.5) | data formatting | bytes 65536
where the time goes:
time: 43.9 us; the launch traced here: 43.6 us
  Pallas kernels  38.6 us (88%)
  local copies, waits for them, and re-layouts  4.41 us (10%)
  between operations  0.64 us (1%)
    pallas_call x1, Pallas kernels, local(): pl.pallas_call(kernel, out_shape=(jax.ShapeDtypeStruct((2, 32, 1024), F32...  38.6 us
    unnamed x3, local copies, waits for them, and re-layouts  4.41 us

commit v1 on v0

v1 whole, which is shorter than its diff:
```python
import functools

import jax
import jax.numpy as jnp
import numpy as np
from jax import lax
from jax.experimental import pallas as pl
from jax.experimental.pallas import tpu as pltpu
from jax.sharding import PartitionSpec as P

MESH = pl.DeviceIdType.MESH
F32, BF16, I16 = jnp.float32, jnp.bfloat16, jnp.int16
TOP = 32767.0


def tables(edge):
    half = edge // 2
    index = np.arange(edge, dtype=np.float64) + 1.0
    sine = np.sqrt(2.0 / (edge + 1)) * np.sin(np.pi * np.outer(index, index) / (edge + 1))
    eigen = 2.0 - 2.0 * np.cos(np.pi * index / (edge + 1))
    perm = np.zeros((2, 256, 256))
    for b8 in range(8):
        for c in range(edge):
            rc, cc = (0, c) if c < half else (1, edge - 1 - c)
            perm[0, b8 * edge + c, rc * 128 + b8 * half + cc] = 1.0
            perm[1, b8 * edge + c, rc * 128 + (7 - b8) * half + cc] = 1.0
    perms = np.concatenate([perm, perm.transpose(0, 2, 1)])
    planes, scales = [], []
    for pb in range(2):
        for pc in range(2):
            planes.append(np.kron(sine[pb::2, :half].T, sine[pc::2, :half].T))
            scales.append(
                1.0
                / (
                    eigen[:, None, None]
                    + eigen[None, pb::2, None]
                    + eigen[None, None, pc::2]
                ).reshape(edge, half * half)
            )
    planes = np.stack(planes)
    both = np.stack([planes, planes.transpose(0, 2, 1)]).astype(np.float32)
    high = both.astype(jnp.bfloat16)
    low = (both - high.astype(np.float32)).astype(jnp.bfloat16)
    weights = np.stack([high, low], axis=2)
    small = np.kron(np.eye(2), sine).astype(np.float32)
    small_high = small.astype(jnp.bfloat16)
    small_low = (small - small_high.astype(np.float32)).astype(jnp.bfloat16)
    rows = np.concatenate([small_high, small_high, small_low, small_low], axis=1)
    return (
        perms.astype(jnp.bfloat16),
        weights,
        rows,
        np.stack(scales).astype(np.float32),
    )


def dot(a, b):
    return jnp.dot(a, b, preferred_element_type=F32)


def split(x):
    high = x.astype(BF16)
    return high, (x - high.astype(F32)).astype(BF16)


def permuted(x, perm_ref):
    halves = []
    for rb in range(2):
        parts = [[None, None], [None, None]]
        for n in range(2):
            m = n if rb == 0 else 3 - n
            y = dot(x[:, m * 256 : (m + 1) * 256], perm_ref[rb])
            parts[0][n], parts[1][n] = y[:, :128], y[:, 128:]
        halves.append(jnp.concatenate(parts[0] + parts[1], axis=1))
    return halves


def restored(halves, perm_ref):
    rows = halves[0].shape[0]
    groups = [None] * 4
    for rb in range(2):
        for n in range(2):
            m = n if rb == 0 else 3 - n
            x = jnp.concatenate(
                [
                    halves[rb][:, n * 128 : (n + 1) * 128],
                    halves[rb][:, 256 + n * 128 : 256 + (n + 1) * 128],
                ],
                axis=1,
            )
            y = dot(jnp.concatenate(split(x), axis=0), perm_ref[2 + rb])
            groups[m] = y[:rows] + y[rows:]
    return jnp.concatenate(groups, axis=1)


def plane(g, weight_ref, way):
    out = []
    for p in range(4):
        high, low = split(g[p])
        rows = high.shape[0]
        a = dot(jnp.concatenate([high, low], axis=0), weight_ref[way, p, 0])
        out.append(a[:rows] + a[rows:] + dot(high, weight_ref[way, p, 1]))
    return out


def along_rows(g, rows):
    out = []
    for p in range(4):
        high, low = split(g[p])
        out.append(dot(rows, jnp.concatenate([high, low, high, low], axis=0)))
    return out


def peak(tiles):
    tiles = [jnp.abs(t) for t in tiles]
    while len(tiles) > 1:
        tiles = [
            jnp.maximum(tiles[i], tiles[i + 1]) if i + 1 < len(tiles) else tiles[i]
            for i in range(0, len(tiles), 2)
        ]
    return jnp.maximum(tiles[0], 1e-30)


def lane_tiles(x):
    return [x[:, j * 128 : (j + 1) * 128] for j in range(x.shape[1] // 128)]


def coded(x, wide):
    return jnp.round(x * wide).astype(jnp.int32)


def spread(tile, times):
    return jnp.concatenate([tile] * times, axis=1)


def kernel(
    res_hbm,
    trav_hbm,
    pair_hbm,
    perm_hbm,
    weight_hbm,
    rows_hbm,
    scale_hbm,
    res_out,
    trav_out,
    res_in,
    trav_in,
    pair_ref,
    perm_ref,
    weight_ref,
    rows_ref,
    scale_ref,
    load_sem,
    mine,
    tbuf,
    ubuf,
    res_acc,
    half,
    other,
    ysum,
    ycode,
    yscale,
    yget,
    ygets,
    hcode,
    hscale,
    hget,
    hgets,
    total,
    res_done,
    trav_done,
    out_sem,
    z_send,
    f_send,
    t_recv,
    x_send,
    x_recv,
    c_send,
    c_recv,
    y_send,
    ys_send,
    y_recv,
    ys_recv,
    h_send,
    hs_send,
    h_recv,
    hs_recv,
):
    n_blk = lax.axis_size("blk")
    blk, grp = lax.axis_index("blk"), lax.axis_index("grp")
    core = lax.rem(blk, 2)
    first = blk - core
    y, lo = grp // 2, lax.rem(grp, 2)
    partner = (first + 1 - core, grp)
    across_z = y * 2 + 1 - lo

    def around(b):
        return lax.rem(b + n_blk, n_blk)

    def y_peer(d):
        return lax.rem(y + d, 4)

    def remote(src, dst, send, recv, to):
        return pltpu.make_async_remote_copy(
            src_ref=src, dst_ref=dst, send_sem=send, recv_sem=recv, device_id=to, device_id_type=MESH
        )

    loads = [
        pltpu.make_async_copy(src, dst, load_sem.at[j])
        for j, (src, dst) in enumerate(
            (
                (trav_hbm, trav_in),
                (perm_hbm, perm_ref),
                (res_hbm, res_in),
                (pair_hbm, pair_ref),
                (rows_hbm, rows_ref),
                (scale_hbm, scale_ref),
                (weight_hbm, weight_ref),
            )
        )
    ]
    for load in loads:
        load.start()

    barrier = pltpu.get_barrier_semaphore()
    near_by = [(first + c, y_peer(d) * 2 + lo) for d in range(1, 4) for c in range(2)]
    near_by += [partner, (blk, across_z)]
    senders = [(around(blk - 4), across_z), (around(blk - 2), across_z)]
    for to in senders + near_by:
        pl.semaphore_signal(barrier, inc=1, device_id=to, device_id_type=MESH)

    loads[0].wait()
    loads[1].wait()
    own = [h.reshape(2, 4, 8, 512) for h in permuted(trav_in[...].reshape(64, 1024), perm_ref)]
    for q in range(4):
        for t in range(2):
            mine[q, t] = jnp.concatenate([own[0][t, q], own[1][t, q]], axis=0).astype(BF16)

    pl.semaphore_wait(barrier, len(senders) + len(near_by))

    hops = []
    for near in range(2):
        slot = near * 2 + core
        hop = remote(
            mine.at[y],
            tbuf.at[slot, y],
            z_send.at[near],
            t_recv.at[slot, y],
            (around(blk + (2 if near else 4)), across_z),
        )
        hop.start()
        hops.append(hop)

    def to_partner(slot, src):
        return remote(src, tbuf.at[slot], x_send.at[slot], x_recv.at[slot], partner)

    @pl.when(core == 0)
    def _():
        to_partner(0, mine).start()

    loads[2].wait()
    for rb, h in enumerate(permuted(res_in[...].reshape(64, 1024), perm_ref)):
        for r in range(2):
            ubuf[r, rb] = h[r * 32 : (r + 1) * 32]
    res_acc[...] = jnp.zeros_like(res_acc)

    def forward(near, d):
        slot = near * 2 + core
        return remote(
            tbuf.at[slot, y],
            tbuf.at[slot, y],
            f_send.at[near, d - 1],
            t_recv.at[slot, y],
            (blk, y_peer(d) * 2 + lo),
        )

    for near in range(2):
        hops[near].wait_recv()
        for d in range(1, 4):
            forward(near, d).start()

    for load in loads[3:]:
        load.wait()

    def to_other(i):
        return remote(half.at[i, 1 - core], other.at[i], c_send.at[i], c_recv.at[i], partner)

    def y_copies(e, d):
        to = (blk, y_peer(d) * 2 + lo)
        return (
            remote(ycode.at[e, y_peer(d)], yget.at[e, d - 1], y_send.at[e, d - 1], y_recv.at[e, d - 1], to),
            remote(
                yscale.at[e, pl.ds(0, 1)],
                ygets.at[e, d - 1, pl.ds(0, 1)],
                ys_send.at[e, d - 1],
                ys_recv.at[e, d - 1],
                to,
            ),
        )

    def h_copies(e):
        to = (around(first - 4 + e), y * 2 + core)
        at = (5 - e) // 2 * 2 + lo
        return (
            remote(hcode.at[e], hget.at[at], h_send.at[e], h_recv.at[at], to),
            remote(hscale.at[e, pl.ds(0, 1)], hgets.at[at, pl.ds(0, 1)], hs_send.at[e], hs_recv.at[at], to),
        )

    def solve(i):
        s = lax.rem(3 - i + core, 4)
        pick = [[pair_ref[0, e, p, s] for e in range(3)] for p in range(2)]
        both = []
        for t in range(2):
            wide = tbuf[i, :, t].astype(F32).reshape(4, 2, 8, 512)
            both.append([wide[:, rb].reshape(32, 512) for rb in range(2)])
        u, w = [], []
        for p in range(2):
            u.append([ubuf[pick[p][0], rb] for rb in range(2)])
            second = pick[p][1] == 1
            w.append([jnp.where(second, both[1][rb], both[0][rb]) for rb in range(2)])
        d = [jnp.concatenate([u[p][rb] * w[p][rb] for p in range(2)], axis=0) for rb in range(2)]
        g = []
        for e in (d[0] + d[1], d[0] - d[1]):
            g += [e[:, :256] + e[:, 256:], e[:, :256] - e[:, 256:]]
        rows = rows_ref[...]
        g = along_rows(plane(g, weight_ref, 0), rows)
        g = [
            (m.reshape(2, 32, 256) * scale_ref[p][None]).reshape(64, 256)
            for p, m in enumerate(g)
        ]
        g = plane(along_rows(g, rows), weight_ref, 1)
        pot = []
        for e, o in (
            (g[0] + g[2], g[1] + g[3]),
            (g[0] - g[2], g[1] - g[3]),
        ):
            pot.append(jnp.concatenate([e + o, e - o], axis=1))

        def factor(p, e, value):
            return jnp.where(pick[p][e] == value, pick[p][2], 0).astype(F32)

        upper = lax.broadcasted_iota(jnp.int32, (4, 8, 512), 1) < 4
        for rb in range(2):
            v = [pot[rb][p * 32 : (p + 1) * 32] for p in range(2)]
            vw = [v[p] * w[p][rb] for p in range(2)]
            vu = [v[p] * u[p][rb] for p in range(2)]
            terms = []
            for j in range(2):
                res_acc[j, rb] += vw[0] * factor(0, 0, j) + vw[1] * factor(1, 0, j)
                terms.append((vu[0] * factor(0, 1, j) + vu[1] * factor(1, 1, j)).reshape(4, 8, 512))
            half[i, 0, :, rb] = jnp.where(upper, terms[0], pltpu.roll(terms[1], 4, 1))
            half[i, 1, :, rb] = jnp.where(upper, pltpu.roll(terms[0], 4, 1), terms[1])

    def one_row(tiles):
        top = jnp.max(peak(tiles), axis=0, keepdims=True)
        return top, jnp.broadcast_to(TOP / top, (8, 128))

    def over_y(e, value):
        ysum[e] = value
        top, wide = one_row([t for q in range(4) for rb in range(2) for t in lane_tiles(value[q, rb])])
        yscale[e, pl.ds(0, 1)] = top * (1.0 / TOP)
        wide = spread(wide, 4)
        for q in range(4):
            ycode[e, q] = jnp.concatenate([coded(value[q, rb], wide) for rb in range(2)], axis=0).astype(I16)
        for d in range(1, 4):
            for copy in y_copies(e, d):
                copy.start()

    def widened(code_ref, scale_row):
        code = code_ref[...].astype(jnp.int32).astype(F32)
        scale = spread(jnp.broadcast_to(scale_row, (8, 128)), 4)
        return [code[rb * 8 : (rb + 1) * 8] * scale for rb in range(2)]

    def homeward(e):
        sums = [ysum[e, y, rb] for rb in range(2)]
        for d in range(1, 4):
            for copy in y_copies(e, d):
                copy.wait_recv()
            for rb, part in enumerate(widened(yget.at[e, d - 1], ygets[e, d - 1, pl.ds(0, 1)])):
                sums[rb] += part
        top, wide = one_row([t for rb in range(2) for t in lane_tiles(sums[rb])])
        hscale[e, pl.ds(0, 1)] = top * (1.0 / TOP)
        wide = spread(wide, 4)
        hcode[e] = jnp.concatenate([coded(sums[rb], wide) for rb in range(2)], axis=0).astype(I16)

    stays = jnp.logical_and(core == 0, lo == 0)

    def step(i, carry):
        @pl.when(i < 2)
        def _():
            slot = i * 2 + core
            for d in range(1, 4):
                q = y_peer(d)
                remote(mine.at[q], tbuf.at[slot, q], z_send.at[0], t_recv.at[slot, q], partner).wait_recv()

            @pl.when(slot > 0)
            def _():
                to_partner(slot, tbuf.at[slot]).start()

        @pl.when(lax.rem(i, 2) != core)
        def _():
            to_partner(i, mine).wait_recv()

        solve(i)
        to_other(i).start()

        @pl.when(i == 0)
        def _():
            over_y(4 * core, half[0, core])

        @pl.when(i == 1)
        def _():
            to_other(0).wait_recv()
            over_y(4 - 4 * core, other[0])

        @pl.when(i > 1)
        def _():
            to_other(i - 1).wait_recv()
            over_y(i - 1, half[i - 1, core] + other[i - 1])

        return carry

    lax.fori_loop(0, 4, step, 0)

    to_other(3).wait_recv()
    over_y(3, half[3, core] + other[3])
    for r in range(2):
        res_done[r] = restored([res_acc[r, rb] for rb in range(2)], perm_ref)
    outs = [
        pltpu.make_async_copy(res_done, res_out, out_sem.at[0]),
        pltpu.make_async_copy(trav_done, trav_out, out_sem.at[1]),
    ]
    outs[0].start()

    def send_home(e, carry):
        homeward(e)
        for copy in h_copies(e):
            copy.start()
        return carry

    lax.fori_loop(0, 4, send_home, 0)
    homeward(4)

    @pl.when(stays)
    def _():
        hget[0] = hcode[4]
        hgets[0, pl.ds(0, 1)] = hscale[4, pl.ds(0, 1)]

    @pl.when(jnp.logical_not(stays))
    def _():
        for copy in h_copies(4):
            copy.start()

    def from_home(at):
        return (
            remote(hcode.at[0], hget.at[at], h_send.at[0], h_recv.at[at], partner),
            remote(hscale.at[0, pl.ds(0, 1)], hgets.at[at, pl.ds(0, 1)], hs_send.at[0], hs_recv.at[at], partner),
        )

    def take(at):
        for rb, part in enumerate(widened(hget.at[at], hgets[at, pl.ds(0, 1)])):
            total[rb] += part

    total[...] = jnp.zeros_like(total)
    for at in range(2, 6):
        for copy in from_home(at):
            copy.wait_recv()
        take(at)

    @pl.when(core == 0)
    def _():
        for at in range(2):
            if at:
                for copy in from_home(at):
                    copy.wait_recv()
            else:

                @pl.when(lo > 0)
                def _():
                    for copy in from_home(0):
                        copy.wait_recv()

            take(at)

    trav_done[...] = restored([total[rb] for rb in range(2)], perm_ref).reshape(2, 4, 1024)
    outs[1].start()

    for near in range(2):
        hops[near].wait_send()
        for d in range(1, 4):
            forward(near, d).wait_send()
    to_partner(2 + core, mine).wait_send()
    to_partner(core, mine).wait_send()
    for i in range(4):
        to_other(i).wait_send()
    for e in range(5):
        for d in range(1, 4):
            for copy in y_copies(e, d):
                copy.wait_send()
        if e < 4:
            for copy in h_copies(e):
                copy.wait_send()

    @pl.when(jnp.logical_not(stays))
    def _():
        for copy in h_copies(4):
            copy.wait_send()

    for out in outs:
        out.wait()


def local(residents, travellers, pair_list):
    consts = tables(32)
    hbm = pl.BlockSpec(memory_space=pltpu.HBM)
    dma = pltpu.SemaphoreType.DMA
    return pl.pallas_call(
        kernel,
        out_shape=(
            jax.ShapeDtypeStruct((2, 32, 1024), F32),
            jax.ShapeDtypeStruct((2, 4, 1024), F32),
        ),
        in_specs=[hbm] * 7,
        out_specs=(hbm, hbm),
        scratch_shapes=[
            pltpu.VMEM((2, 32, 1024), BF16),
            pltpu.VMEM((2, 32, 1024), BF16),
            pltpu.SMEM((1, 3, 2, 4), jnp.int32),
            pltpu.VMEM((4, 256, 256), BF16),
            pltpu.VMEM((2, 4, 2, 256, 256), BF16),
            pltpu.VMEM((64, 256), BF16),
            pltpu.VMEM((4, 32, 256), F32),
            dma((7,)),
            pltpu.VMEM((4, 2, 16, 512), BF16),
            pltpu.VMEM((4, 4, 2, 16, 512), BF16),
            pltpu.VMEM((2, 2, 32, 512), F32),
            pltpu.VMEM((2, 2, 32, 512), F32),
            pltpu.VMEM((4, 2, 4, 2, 8, 512), F32),
            pltpu.VMEM((4, 4, 2, 8, 512), F32),
            pltpu.VMEM((5, 4, 2, 8, 512), F32),
            pltpu.VMEM((5, 4, 16, 512), I16),
            pltpu.VMEM((5, 8, 128), F32),
            pltpu.VMEM((5, 3, 16, 512), I16),
            pltpu.VMEM((5, 3, 8, 128), F32),
            pltpu.VMEM((5, 16, 512), I16),
            pltpu.VMEM((5, 8, 128), F32),
            pltpu.VMEM((6, 16, 512), I16),
            pltpu.VMEM((6, 8, 128), F32),
            pltpu.VMEM((2, 8, 512), F32),
            pltpu.VMEM((2, 32, 1024), F32),
            pltpu.VMEM((2, 4, 1024), F32),
            dma((2,)),
            dma((2,)),
            dma((2, 3)),
            dma((4, 4)),
            dma((4,)),
            dma((4,)),
            dma((4,)),
            dma((4,)),
            dma((5, 3)),
            dma((5, 3)),
            dma((5, 3)),
            dma((5, 3)),
            dma((5,)),
            dma((5,)),
            dma((6,)),
            dma((6,)),
        ],
        compiler_params=pltpu.CompilerParams(
            collective_id=0, has_side_effects=True
        ),
    )(residents, travellers, pair_list.transpose(0, 3, 2, 1), *[jnp.asarray(c) for c in consts])


def solution(mesh):
    return jax.shard_map(
        local,
        mesh=mesh,
        in_specs=(
            P(("blk", "grp"), None, None),
            P("blk", None, None),
            P(("blk", "grp"), None, None, None),
        ),
        out_specs=(P(("blk", "grp"), None, None), P("blk", "grp", None)),
        check_vma=False,
    )
```

time: 43.9 us -> 38.6 us (0.88)
  Pallas kernels: 38.6 us -> 34.7 us
  local copies, waits for them, and re-layouts: 4.41 us -> 3.05 us
    pallas_call x1, Pallas kernels: 38.6 us -> 34.7 us  [local(): pl.pallas_call(kernel, out_shape=(jax.ShapeDtypeStruct((2, 32, 1024), F32...]
    unnamed x3 -> x2, local copies, waits for them, and re-layouts: 4.41 us -> 3.05 us
where the time goes in v1:
time: 38.6 us; the launch traced here: 38.4 us
  Pallas kernels  34.7 us (90%)
  local copies, waits for them, and re-layouts  3.05 us (8%)
  between operations  0.64 us (2%)
    pallas_call x1, Pallas kernels, local(): pl.pallas_call(kernel, out_shape=(jax.ShapeDtypeStruct((2, 32, 1024), F32...  34.7 us
    unnamed x2, local copies, waits for them, and re-layouts  3.05 us

profile of v1, /device:TPU:1, one launch (start us, length us, event | category | flops | bytes accessed | tf_op | source)
XLA Modules:
  0.0 38.4 jit_solution(10083894678640135538)
XLA Ops:
  0.6 34.7 %shard_map.86 = (f32[2,32,1024]{2,1,0:T(8,128)}, f32[2,4,1024]{2,1,0:T(4,128)}) custom-call(bf16[2,32,1024]{2,1,0:T(8,128)(2,1)} %res_hbm.1, bf16[2,32,1024]{2,1,0:T(8,128)(2,1)} %trav_hbm.1, s32[1,3,2,4]{3,2,1,0:T(2,128)} %bitcast.1, bf16[4,256,256]{2,1,0:T(8,128)(2,1)} %constant.8.clone.perm_hbm, bf16[2,4,2,256,256]{4,3,2,1,0:T(8,128)(2,1)} %constant.9.clone.weight_hbm, ...), custom_call_target="tpu_custom_call" | custom-call | tf_op jit(solution)/shard_map/pallas_call | solution.py:517
  35.4 1.7 %copy.11 = f32[2,32,1024]{2,1,0:T(8,128)} copy(f32[2,32,1024]{2,1,0:T(8,128)} %get-tuple-element.4) | data formatting | bytes 524288
  37.1 1.4 %copy.12 = f32[2,4,1024]{2,1,0:T(4,128)} copy(f32[2,4,1024]{2,1,0:T(4,128)} %get-tuple-element.5) | data formatting | bytes 65536

commit v2 on v1

--- a/solution.py
+++ b/solution.py
@@ -155,7 +155,7 @@
     tbuf,
     ubuf,
     res_acc,
-    half,
+    terms,
     other,
     ysum,
     ycode,
@@ -167,9 +167,6 @@
     hget,
     hgets,
     total,
-    res_done,
-    trav_done,
-    out_sem,
     z_send,
     f_send,
     t_recv,
@@ -223,9 +220,8 @@
         load.start()
 
     barrier = pltpu.get_barrier_semaphore()
-    near_by = [(first + c, y_peer(d) * 2 + lo) for d in range(1, 4) for c in range(2)]
-    near_by += [partner, (blk, across_z)]
-    senders = [(around(blk - 4), across_z), (around(blk - 2), across_z)]
+    near_by = [(blk, y_peer(d) * 2 + lo) for d in range(1, 4)] + [partner, (blk, across_z)]
+    senders = [(around(blk - 4), across_z), (around(blk - 2), grp)]
     for to in senders + near_by:
         pl.semaphore_signal(barrier, inc=1, device_id=to, device_id_type=MESH)
 
@@ -246,7 +242,7 @@
             tbuf.at[slot, y],
             z_send.at[near],
             t_recv.at[slot, y],
-            (around(blk + (2 if near else 4)), across_z),
+            (around(blk + 2), grp) if near else (around(blk + 4), across_z),
         )
         hop.start()
         hops.append(hop)
@@ -274,16 +270,11 @@
             (blk, y_peer(d) * 2 + lo),
         )
 
-    for near in range(2):
-        hops[near].wait_recv()
-        for d in range(1, 4):
-            forward(near, d).start()
-
     for load in loads[3:]:
         load.wait()
 
-    def to_other(i):
-        return remote(half.at[i, 1 - core], other.at[i], c_send.at[i], c_recv.at[i], partner)
+    def to_other(slot):
+        return remote(terms.at[slot], other.at[slot], c_send.at[slot], c_recv.at[slot], partner)
 
     def y_copies(e, d):
         to = (blk, y_peer(d) * 2 + lo)
@@ -299,12 +290,15 @@
         )
 
     def h_copies(e):
-        to = (around(first - 4 + e), y * 2 + core)
         at = (5 - e) // 2 * 2 + lo
-        return (
-            remote(hcode.at[e], hget.at[at], h_send.at[e], h_recv.at[at], to),
-            remote(hscale.at[e, pl.ds(0, 1)], hgets.at[at, pl.ds(0, 1)], hs_send.at[e], hs_recv.at[at], to),
-        )
+        copies = []
+        for z in range(2):
+            to = (around(first - 4 + e), y * 2 + z)
+            copies += [
+                remote(hcode.at[e, z], hget.at[at], h_send.at[e, z], h_recv.at[at], to),
+                remote(hscale.at[e, pl.ds(0, 1)], hgets.at[at, pl.ds(0, 1)], hs_send.at[e, z], hs_recv.at[at], to),
+            ]
+        return copies
 
     def solve(i):
         s = lax.rem(3 - i + core, 4)
@@ -339,17 +333,13 @@
         def factor(p, e, value):
             return jnp.where(pick[p][e] == value, pick[p][2], 0).astype(F32)
 
-        upper = lax.broadcasted_iota(jnp.int32, (4, 8, 512), 1) < 4
         for rb in range(2):
             v = [pot[rb][p * 32 : (p + 1) * 32] for p in range(2)]
             vw = [v[p] * w[p][rb] for p in range(2)]
             vu = [v[p] * u[p][rb] for p in range(2)]
-            terms = []
             for j in range(2):
                 res_acc[j, rb] += vw[0] * factor(0, 0, j) + vw[1] * factor(1, 0, j)
-                terms.append((vu[0] * factor(0, 1, j) + vu[1] * factor(1, 1, j)).reshape(4, 8, 512))
-            half[i, 0, :, rb] = jnp.where(upper, terms[0], pltpu.roll(terms[1], 4, 1))
-            half[i, 1, :, rb] = jnp.where(upper, pltpu.roll(terms[0], 4, 1), terms[1])
+                terms[i, :, j, rb] = (vu[0] * factor(0, 1, j) + vu[1] * factor(1, 1, j)).reshape(4, 8, 512)
 
     def one_row(tiles):
         top = jnp.max(peak(tiles), axis=0, keepdims=True)
@@ -357,11 +347,13 @@
 
     def over_y(e, value):
         ysum[e] = value
-        top, wide = one_row([t for q in range(4) for rb in range(2) for t in lane_tiles(value[q, rb])])
+        parts = [(q, t, rb) for q in range(4) for t in range(2) for rb in range(2)]
+        top, wide = one_row([x for at in parts for x in lane_tiles(value[at])])
         yscale[e, pl.ds(0, 1)] = top * (1.0 / TOP)
         wide = spread(wide, 4)
         for q in range(4):
-            ycode[e, q] = jnp.concatenate([coded(value[q, rb], wide) for rb in range(2)], axis=0).astype(I16)
+            for t in range(2):
+                ycode[e, q, t] = jnp.concatenate([coded(value[q, t, rb], wide) for rb in range(2)], axis=0).astype(I16)
         for d in range(1, 4):
             for copy in y_copies(e, d):
                 copy.start()
@@ -372,23 +364,46 @@
         return [code[rb * 8 : (rb + 1) * 8] * scale for rb in range(2)]
 
     def homeward(e):
-        sums = [ysum[e, y, rb] for rb in range(2)]
+        sums = [[ysum[e, y, t, rb] for rb in range(2)] for t in range(2)]
         for d in range(1, 4):
             for copy in y_copies(e, d):
                 copy.wait_recv()
-            for rb, part in enumerate(widened(yget.at[e, d - 1], ygets[e, d - 1, pl.ds(0, 1)])):
-                sums[rb] += part
-        top, wide = one_row([t for rb in range(2) for t in lane_tiles(sums[rb])])
+            for t in range(2):
+                for rb, part in enumerate(widened(yget.at[e, d - 1, t], ygets[e, d - 1, pl.ds(0, 1)])):
+                    sums[t][rb] += part
+        upper = lax.broadcasted_iota(jnp.int32, (8, 512), 0) < 4
+        rows = [
+            [jnp.where(upper, sums[0][rb], pltpu.roll(sums[1][rb], 4, 0)) for rb in range(2)],
+            [jnp.where(upper, pltpu.roll(sums[0][rb], 4, 0), sums[1][rb]) for rb in range(2)],
+        ]
+        top, wide = one_row([x for z in range(2) for rb in range(2) for x in lane_tiles(rows[z][rb])])
         hscale[e, pl.ds(0, 1)] = top * (1.0 / TOP)
         wide = spread(wide, 4)
-        hcode[e] = jnp.concatenate([coded(sums[rb], wide) for rb in range(2)], axis=0).astype(I16)
-
-    stays = jnp.logical_and(core == 0, lo == 0)
+        for z in range(2):
+            hcode[e, z] = jnp.concatenate([coded(rows[z][rb], wide) for rb in range(2)], axis=0).astype(I16)
+        for copy in h_copies(e):
+            copy.start()
+
+    def slot_at(i):
+        return (1 - core) * (lax.rem(2 * i, 3) + i // 3 * 3) + core * (i + i // 2 - i // 3 * 2)
+
+    def entry_of(slot):
+        return slot + 4 * core * (1 - (slot + 3) // 4)
 
     def step(i, carry):
-        @pl.when(i < 2)
-        def _():
-            slot = i * 2 + core
+        slot = slot_at(i)
+
+        @pl.when(i == core)
+        def _():
+            for near in range(2):
+                hops[near].wait_recv()
+                for d in range(1, 4):
+                    forward(near, d).start()
+
+        own = jnp.logical_or(i == core, i == core + 1)
+
+        @pl.when(own)
+        def _():
             for d in range(1, 4):
                 q = y_peer(d)
                 remote(mine.at[q], tbuf.at[slot, q], z_send.at[0], t_recv.at[slot, q], partner).wait_recv()
@@ -397,64 +412,49 @@
             def _():
                 to_partner(slot, tbuf.at[slot]).start()
 
-        @pl.when(lax.rem(i, 2) != core)
-        def _():
-            to_partner(i, mine).wait_recv()
-
-        solve(i)
-        to_other(i).start()
+        @pl.when(jnp.logical_not(own))
+        def _():
+            to_partner(slot, mine).wait_recv()
+
+        solve(slot)
+        gives = jnp.logical_or(i == 1, jnp.logical_and(i == 2, core == 1))
+
+        @pl.when(gives)
+        def _():
+            to_other(slot).start()
 
         @pl.when(i == 0)
         def _():
-            over_y(4 * core, half[0, core])
-
-        @pl.when(i == 1)
-        def _():
-            to_other(0).wait_recv()
-            over_y(4 - 4 * core, other[0])
-
-        @pl.when(i > 1)
-        def _():
-            to_other(i - 1).wait_recv()
-            over_y(i - 1, half[i - 1, core] + other[i - 1])
+            over_y(4 * core, terms[0])
+
+        @pl.when(jnp.logical_and(i > 0, jnp.logical_not(gives)))
+        def _():
+            to_other(slot).wait_recv()
+            over_y(slot, terms[slot] + other[slot])
 
         return carry
 
     lax.fori_loop(0, 4, step, 0)
 
-    to_other(3).wait_recv()
-    over_y(3, half[3, core] + other[3])
     for r in range(2):
-        res_done[r] = restored([res_acc[r, rb] for rb in range(2)], perm_ref)
-    outs = [
-        pltpu.make_async_copy(res_done, res_out, out_sem.at[0]),
-        pltpu.make_async_copy(trav_done, trav_out, out_sem.at[1]),
-    ]
-    outs[0].start()
-
-    def send_home(e, carry):
-        homeward(e)
-        for copy in h_copies(e):
-            copy.start()
+        res_out[r] = restored([res_acc[r, rb] for rb in range(2)], perm_ref)
+
+    def entry_at(j):
+        return (1 - core) * (j + j // 2) + core * (4 - 2 * j)
+
+    def send_home(j, carry):
+        @pl.when(j < 3 - core)
+        def _():
+            homeward(entry_at(j))
+
         return carry
 
-    lax.fori_loop(0, 4, send_home, 0)
-    homeward(4)
-
-    @pl.when(stays)
-    def _():
-        hget[0] = hcode[4]
-        hgets[0, pl.ds(0, 1)] = hscale[4, pl.ds(0, 1)]
-
-    @pl.when(jnp.logical_not(stays))
-    def _():
-        for copy in h_copies(4):
-            copy.start()
+    lax.fori_loop(0, 3, send_home, 0)
 
     def from_home(at):
         return (
-            remote(hcode.at[0], hget.at[at], h_send.at[0], h_recv.at[at], partner),
-            remote(hscale.at[0, pl.ds(0, 1)], hgets.at[at, pl.ds(0, 1)], hs_send.at[0], hs_recv.at[at], partner),
+            remote(hcode.at[0, 0], hget.at[at], h_send.at[0, 0], h_recv.at[at], partner),
+            remote(hscale.at[0, pl.ds(0, 1)], hgets.at[at, pl.ds(0, 1)], hs_send.at[0, 0], hs_recv.at[at], partner),
         )
 
     def take(at):
@@ -470,20 +470,11 @@
     @pl.when(core == 0)
     def _():
         for at in range(2):
-            if at:
-                for copy in from_home(at):
-                    copy.wait_recv()
-            else:
-
-                @pl.when(lo > 0)
-                def _():
-                    for copy in from_home(0):
-                        copy.wait_recv()
-
+            for copy in from_home(at):
+                copy.wait_recv()
             take(at)
 
-    trav_done[...] = restored([total[rb] for rb in range(2)], perm_ref).reshape(2, 4, 1024)
-    outs[1].start()
+    trav_out[...] = restored([total[rb] for rb in range(2)], perm_ref).reshape(2, 4, 1024)
 
     for near in range(2):
         hops[near].wait_send()
@@ -491,37 +482,47 @@
             forward(near, d).wait_send()
     to_partner(2 + core, mine).wait_send()
     to_partner(core, mine).wait_send()
-    for i in range(4):
-        to_other(i).wait_send()
-    for e in range(5):
-        for d in range(1, 4):
-            for copy in y_copies(e, d):
+    to_other(2 - core).wait_send()
+
+    @pl.when(core == 1)
+    def _():
+        to_other(3).wait_send()
+
+    def sent(j, carry):
+        @pl.when(j < 3 - core)
+        def _():
+            for d in range(1, 4):
+                for copy in y_copies(entry_at(j), d):
+                    copy.wait_send()
+            for copy in h_copies(entry_at(j)):
                 copy.wait_send()
-        if e < 4:
-            for copy in h_copies(e):
-                copy.wait_send()
-
-    @pl.when(jnp.logical_not(stays))
-    def _():
-        for copy in h_copies(4):
-            copy.wait_send()
-
-    for out in outs:
-        out.wait()
+
+        return carry
+
+    lax.fori_loop(0, 3, sent, 0)
+
+
+def store(res_ref, trav_ref, res_out, trav_out, sem):
+    copies = [
+        pltpu.make_async_copy(res_ref, res_out, sem.at[0]),
+        pltpu.make_async_copy(trav_ref, trav_out, sem.at[1]),
+    ]
+    for copy in copies:
+        copy.start()
+    for copy in copies:
+        copy.wait()
 
 
 def local(residents, travellers, pair_list):
     consts = tables(32)
     hbm = pl.BlockSpec(memory_space=pltpu.HBM)
+    vmem = pl.BlockSpec(memory_space=pltpu.VMEM)
     dma = pltpu.SemaphoreType.DMA
-    return pl.pallas_call(
+    done = pl.pallas_call(
         kernel,
-        out_shape=(
-            jax.ShapeDtypeStruct((2, 32, 1024), F32),
-            jax.ShapeDtypeStruct((2, 4, 1024), F32),
-        ),
+        out_shape=(pltpu.VMEM((2, 32, 1024), F32), pltpu.VMEM((2, 4, 1024), F32)),
         in_specs=[hbm] * 7,
-        out_specs=(hbm, hbm),
+        out_specs=(vmem, vmem),
         scratch_shapes=[
             pltpu.VMEM((2, 32, 1024), BF16),
             pltpu.VMEM((2, 32, 1024), BF16),
@@ -535,21 +536,18 @@
             pltpu.VMEM((4, 4, 2, 16, 512), BF16),
             pltpu.VMEM((2, 2, 32, 512), F32),
             pltpu.VMEM((2, 2, 32, 512), F32),
-            pltpu.VMEM((4, 2, 4, 2, 8, 512), F32),
-            pltpu.VMEM((4, 4, 2, 8, 512), F32),
-            pltpu.VMEM((5, 4, 2, 8, 512), F32),
-            pltpu.VMEM((5, 4, 16, 512), I16),
+            pltpu.VMEM((4, 4, 2, 2, 8, 512), F32),
+            pltpu.VMEM((4, 4, 2, 2, 8, 512), F32),
+            pltpu.VMEM((5, 4, 2, 2, 8, 512), F32),
+            pltpu.VMEM((5, 4, 2, 16, 512), I16),
             pltpu.VMEM((5, 8, 128), F32),
-            pltpu.VMEM((5, 3, 16, 512), I16),
+            pltpu.VMEM((5, 3, 2, 16, 512), I16),
             pltpu.VMEM((5, 3, 8, 128), F32),
-            pltpu.VMEM((5, 16, 512), I16),
+            pltpu.VMEM((5, 2, 16, 512), I16),
             pltpu.VMEM((5, 8, 128), F32),
             pltpu.VMEM((6, 16, 512), I16),
             pltpu.VMEM((6, 8, 128), F32),
             pltpu.VMEM((2, 8, 512), F32),
-            pltpu.VMEM((2, 32, 1024), F32),
-            pltpu.VMEM((2, 4, 1024), F32),
-            dma((2,)),
             dma((2,)),
             dma((2, 3)),
             dma((4, 4)),
@@ -561,8 +559,8 @@
             dma((5, 3)),
             dma((5, 3)),
             dma((5, 3)),
-            dma((5,)),
-            dma((5,)),
+            dma((5, 2)),
+            dma((5, 2)),
             dma((6,)),
             dma((6,)),
         ],
@@ -570,6 +568,17 @@
             collective_id=0, has_side_effects=True
         ),
     )(residents, travellers, pair_list.transpose(0, 3, 2, 1), *[jnp.asarray(c) for c in consts])
+    return pl.pallas_call(
+        store,
+        out_shape=(
+            jax.ShapeDtypeStruct((2, 32, 1024), F32),
+            jax.ShapeDtypeStruct((2, 4, 1024), F32),
+        ),
+        in_specs=[vmem] * 2,
+        out_specs=(hbm, hbm),
+        scratch_shapes=[dma((2,))],
+        compiler_params=pltpu.CompilerParams(vmem_limit_bytes=2**20),
+    )(*done)
 
 
 def solution(mesh):

time: 38.6 us -> 34.7 us (0.90)
  local copies, waits for them, and re-layouts: 3.05 us -> 0 us
  Pallas kernels: 34.7 us -> 34 us
    unnamed x2 -> x0, local copies, waits for them, and re-layouts: 3.05 us -> none
    pallas_call x1 -> x2, Pallas kernels: 34.7 us -> 34 us  [the longest x1 33.2 us: local(): pl.pallas_call(kernel, out_shape=(pltpu.VMEM((2, 32, 1024), F32), pltpu.V...]
where the time goes in v2:
time: 34.7 us; the launch traced here: 34.6 us
  Pallas kernels  34 us (98%)
  between operations  0.64 us (2%)
    pallas_call x1, Pallas kernels, local(): pl.pallas_call(kernel, out_shape=(pltpu.VMEM((2, 32, 1024), F32), pltpu.V...  33.2 us
    pallas_call x1, Pallas kernels, local(): pl.pallas_call(store, out_shape=(jax.ShapeDtypeStruct((2, 32, 1024), F32)...  0.72 us

profile of v2, /device:TPU:1, one launch (start us, length us, event | category | flops | bytes accessed | tf_op | source)
XLA Modules:
  0.0 34.6 jit_solution(16924011782843720835)
XLA Ops:
  0.6 33.2 %shard_map.86 = (f32[2,32,1024]{2,1,0:T(8,128)S(1)}, f32[2,4,1024]{2,1,0:T(4,128)S(1)}) custom-call(bf16[2,32,1024]{2,1,0:T(8,128)(2,1)} %res_hbm.1, bf16[2,32,1024]{2,1,0:T(8,128)(2,1)} %trav_hbm.1, s32[1,3,2,4]{3,2,1,0:T(2,128)} %bitcast.1, bf16[4,256,256]{2,1,0:T(8,128)(2,1)} %constant.8.clone.perm_hbm, ...), custom_call_target="tpu_custom_call" | custom-call | tf_op jit(solution)/shard_map/pallas_call | solution.py:521
  33.9 0.7 %shard_map.87 = (f32[2,32,1024]{2,1,0:T(8,128)}, f32[2,4,1024]{2,1,0:T(4,128)}) custom-call(f32[2,32,1024]{2,1,0:T(8,128)S(1)} %get-tuple-element.4.res_ref, f32[2,4,1024]{2,1,0:T(4,128)S(1)} %get-tuple-element.5.trav_ref), custom_call_target="tpu_custom_call" | custom-call | tf_op jit(solution)/shard_map/pallas_call | solution.py:571

commit v3 on v2

--- a/solution.py
+++ b/solution.py
@@ -157,7 +157,6 @@
     res_acc,
     terms,
     other,
-    ysum,
     ycode,
     yscale,
     yget,
@@ -220,10 +219,20 @@
         load.start()
 
     barrier = pltpu.get_barrier_semaphore()
-    near_by = [(blk, y_peer(d) * 2 + lo) for d in range(1, 4)] + [partner, (blk, across_z)]
-    senders = [(around(blk - 4), across_z), (around(blk - 2), grp)]
-    for to in senders + near_by:
+
+    def arrive(to):
         pl.semaphore_signal(barrier, inc=1, device_id=to, device_id_type=MESH)
+
+    arrive(partner)
+    arrive((blk, across_z))
+
+    @pl.when(core == 1)
+    def _():
+        for c in range(2):
+            arrive((around(first - 4 + c), across_z))
+            arrive((around(first - 2 + c), grp))
+            for d in range(1, 4):
+                arrive((first + c, y_peer(d) * 2 + lo))
 
     loads[0].wait()
     loads[1].wait()
@@ -232,7 +241,7 @@
         for t in range(2):
             mine[q, t] = jnp.concatenate([own[0][t, q], own[1][t, q]], axis=0).astype(BF16)
 
-    pl.semaphore_wait(barrier, len(senders) + len(near_by))
+    pl.semaphore_wait(barrier, 7)
 
     hops = []
     for near in range(2):
@@ -242,7 +251,7 @@
             tbuf.at[slot, y],
             z_send.at[near],
             t_recv.at[slot, y],
-            (around(blk + 2), grp) if near else (around(blk + 4), across_z),
+            (around(first + 3), grp) if near else (around(first + 5), across_z),
         )
         hop.start()
         hops.append(hop)
@@ -252,7 +261,7 @@
 
     @pl.when(core == 0)
     def _():
-        to_partner(0, mine).start()
+        to_partner(4, mine).start()
 
     loads[2].wait()
     for rb, h in enumerate(permuted(res_in[...].reshape(64, 1024), perm_ref)):
@@ -260,12 +269,17 @@
             ubuf[r, rb] = h[r * 32 : (r + 1) * 32]
     res_acc[...] = jnp.zeros_like(res_acc)
 
-    def forward(near, d):
-        slot = near * 2 + core
+    for e in (0, 4):
+        other[e] = jnp.zeros((4, 2, 2, 8, 512), F32)
+
+    def quarter(slot, q):
+        return remote(mine.at[q], tbuf.at[slot, q], z_send.at[0], t_recv.at[slot, q], partner)
+
+    def forward(slot, d):
         return remote(
             tbuf.at[slot, y],
             tbuf.at[slot, y],
-            f_send.at[near, d - 1],
+            f_send.at[slot, d - 1],
             t_recv.at[slot, y],
             (blk, y_peer(d) * 2 + lo),
         )
@@ -277,14 +291,14 @@
         return remote(terms.at[slot], other.at[slot], c_send.at[slot], c_recv.at[slot], partner)
 
     def y_copies(e, d):
-        to = (blk, y_peer(d) * 2 + lo)
+        to = (first + 1, y_peer(d) * 2 + lo)
         return (
-            remote(ycode.at[e, y_peer(d)], yget.at[e, d - 1], y_send.at[e, d - 1], y_recv.at[e, d - 1], to),
+            remote(ycode.at[e, y_peer(d)], yget.at[e, d], y_send.at[e, d], y_recv.at[e, d], to),
             remote(
                 yscale.at[e, pl.ds(0, 1)],
-                ygets.at[e, d - 1, pl.ds(0, 1)],
-                ys_send.at[e, d - 1],
-                ys_recv.at[e, d - 1],
+                ygets.at[e, d, pl.ds(0, 1)],
+                ys_send.at[e, d],
+                ys_recv.at[e, d],
                 to,
             ),
         )
@@ -346,7 +360,6 @@
         return top, jnp.broadcast_to(TOP / top, (8, 128))
 
     def over_y(e, value):
-        ysum[e] = value
         parts = [(q, t, rb) for q in range(4) for t in range(2) for rb in range(2)]
         top, wide = one_row([x for at in parts for x in lane_tiles(value[at])])
         yscale[e, pl.ds(0, 1)] = top * (1.0 / TOP)
@@ -358,18 +371,33 @@
             for copy in y_copies(e, d):
                 copy.start()
 
+        @pl.when(core == 0)
+        def _():
+            for copy in y_copies(e, 0):
+                copy.start()
+
+        @pl.when(core == 1)
+        def _():
+            yget[4, 0] = ycode[4, y]
+            ygets[4, 0, pl.ds(0, 1)] = yscale[4, pl.ds(0, 1)]
+
     def widened(code_ref, scale_row):
         code = code_ref[...].astype(jnp.int32).astype(F32)
         scale = spread(jnp.broadcast_to(scale_row, (8, 128)), 4)
         return [code[rb * 8 : (rb + 1) * 8] * scale for rb in range(2)]
 
     def homeward(e):
-        sums = [[ysum[e, y, t, rb] for rb in range(2)] for t in range(2)]
+        @pl.when(e < 4)
+        def _():
+            for copy in y_copies(e, 0):
+                copy.wait_recv()
+
+        sums = [widened(yget.at[e, 0, t], ygets[e, 0, pl.ds(0, 1)]) for t in range(2)]
         for d in range(1, 4):
             for copy in y_copies(e, d):
                 copy.wait_recv()
             for t in range(2):
-                for rb, part in enumerate(widened(yget.at[e, d - 1, t], ygets[e, d - 1, pl.ds(0, 1)])):
+                for rb, part in enumerate(widened(yget.at[e, d, t], ygets[e, d, pl.ds(0, 1)])):
                     sums[t][rb] += part
         upper = lax.broadcasted_iota(jnp.int32, (8, 512), 0) < 4
         rows = [
@@ -384,52 +412,48 @@
         for copy in h_copies(e):
             copy.start()
 
-    def slot_at(i):
-        return (1 - core) * (lax.rem(2 * i, 3) + i // 3 * 3) + core * (i + i // 2 - i // 3 * 2)
-
-    def entry_of(slot):
-        return slot + 4 * core * (1 - (slot + 3) // 4)
+    def first_order(i):
+        return (1 - i // 2) * (1 - i) + i // 2 * i
+
+    def spread_slots(slots):
+        for slot in slots:
+            for d in range(1, 4):
+                quarter(slot, y_peer(d)).wait_recv()
+            to_partner(slot, tbuf.at[slot]).start()
 
     def step(i, carry):
-        slot = slot_at(i)
-
-        @pl.when(i == core)
-        def _():
-            for near in range(2):
-                hops[near].wait_recv()
+        slot = (1 - core) * first_order(i) + core * (i + 4 * (1 - (i + 3) // 4))
+
+        @pl.when(jnp.logical_and(core == 1, i == 1))
+        def _():
+            for s in (1, 0, 3, 2):
+                quarter(s, y).wait_recv()
                 for d in range(1, 4):
-                    forward(near, d).start()
-
-        own = jnp.logical_or(i == core, i == core + 1)
-
-        @pl.when(own)
-        def _():
-            for d in range(1, 4):
-                q = y_peer(d)
-                remote(mine.at[q], tbuf.at[slot, q], z_send.at[0], t_recv.at[slot, q], partner).wait_recv()
-
-            @pl.when(slot > 0)
-            def _():
-                to_partner(slot, tbuf.at[slot]).start()
-
-        @pl.when(jnp.logical_not(own))
+                    forward(s, d).start()
+            spread_slots((1, 0))
+
+        @pl.when(jnp.logical_and(core == 1, i == 2))
+        def _():
+            spread_slots((2, 3))
+
+        takes = jnp.logical_or(core == 0, i == 0)
+
+        @pl.when(takes)
         def _():
             to_partner(slot, mine).wait_recv()
 
         solve(slot)
-        gives = jnp.logical_or(i == 1, jnp.logical_and(i == 2, core == 1))
-
-        @pl.when(gives)
+
+        @pl.when(jnp.logical_not(takes))
         def _():
             to_other(slot).start()
 
-        @pl.when(i == 0)
-        def _():
-            over_y(4 * core, terms[0])
-
-        @pl.when(jnp.logical_and(i > 0, jnp.logical_not(gives)))
+        @pl.when(jnp.logical_and(core == 0, slot > 0))
         def _():
             to_other(slot).wait_recv()
+
+        @pl.when(takes)
+        def _():
             over_y(slot, terms[slot] + other[slot])
 
         return carry
@@ -440,16 +464,16 @@
         res_out[r] = restored([res_acc[r, rb] for rb in range(2)], perm_ref)
 
     def entry_at(j):
-        return (1 - core) * (j + j // 2) + core * (4 - 2 * j)
+        later = (j + 4) // 5
+        return 4 * (1 - later) + later * first_order(j - later)
 
     def send_home(j, carry):
-        @pl.when(j < 3 - core)
-        def _():
-            homeward(entry_at(j))
-
+        homeward(entry_at(j))
         return carry
 
-    lax.fori_loop(0, 3, send_home, 0)
+    @pl.when(core == 1)
+    def _():
+        lax.fori_loop(0, 5, send_home, 0)
 
     def from_home(at):
         return (
@@ -478,28 +502,31 @@
 
     for near in range(2):
         hops[near].wait_send()
-        for d in range(1, 4):
-            forward(near, d).wait_send()
-    to_partner(2 + core, mine).wait_send()
-    to_partner(core, mine).wait_send()
-    to_other(2 - core).wait_send()
+    for d in range(1, 4):
+        for copy in y_copies(4 * core, d):
+            copy.wait_send()
+
+    @pl.when(core == 0)
+    def _():
+        to_partner(4, mine).wait_send()
+        for e in range(4):
+            for d in range(4):
+                if e == 0 and d > 0:
+                    continue
+                for copy in y_copies(e, d):
+                    copy.wait_send()
 
     @pl.when(core == 1)
     def _():
-        to_other(3).wait_send()
-
-    def sent(j, carry):
-        @pl.when(j < 3 - core)
-        def _():
+        for slot in range(4):
             for d in range(1, 4):
-                for copy in y_copies(entry_at(j), d):
-                    copy.wait_send()
-            for copy in h_copies(entry_at(j)):
+                forward(slot, d).wait_send()
+            to_partner(slot, mine).wait_send()
+            if slot:
+                to_other(slot).wait_send()
+        for e in range(5):
+            for copy in h_copies(e):
                 copy.wait_send()
-
-        return carry
-
-    lax.fori_loop(0, 3, sent, 0)
 
 
 def store(res_ref, trav_ref, res_out, trav_out, sem):
@@ -533,32 +560,31 @@
             pltpu.VMEM((4, 32, 256), F32),
             dma((7,)),
             pltpu.VMEM((4, 2, 16, 512), BF16),
-            pltpu.VMEM((4, 4, 2, 16, 512), BF16),
+            pltpu.VMEM((5, 4, 2, 16, 512), BF16),
             pltpu.VMEM((2, 2, 32, 512), F32),
             pltpu.VMEM((2, 2, 32, 512), F32),
-            pltpu.VMEM((4, 4, 2, 2, 8, 512), F32),
-            pltpu.VMEM((4, 4, 2, 2, 8, 512), F32),
+            pltpu.VMEM((5, 4, 2, 2, 8, 512), F32),
             pltpu.VMEM((5, 4, 2, 2, 8, 512), F32),
             pltpu.VMEM((5, 4, 2, 16, 512), I16),
             pltpu.VMEM((5, 8, 128), F32),
-            pltpu.VMEM((5, 3, 2, 16, 512), I16),
-            pltpu.VMEM((5, 3, 8, 128), F32),
+            pltpu.VMEM((5, 4, 2, 16, 512), I16),
+            pltpu.VMEM((5, 4, 8, 128), F32),
             pltpu.VMEM((5, 2, 16, 512), I16),
             pltpu.VMEM((5, 8, 128), F32),
             pltpu.VMEM((6, 16, 512), I16),
             pltpu.VMEM((6, 8, 128), F32),
             pltpu.VMEM((2, 8, 512), F32),
             dma((2,)),
-            dma((2, 3)),
+            dma((4, 3)),
             dma((4, 4)),
+            dma((5,)),
+            dma((5,)),
             dma((4,)),
             dma((4,)),
-            dma((4,)),
-            dma((4,)),
-            dma((5, 3)),
-            dma((5, 3)),
-            dma((5, 3)),
-            dma((5, 3)),
+            dma((5, 4)),
+            dma((5, 4)),
+            dma((5, 4)),
+            dma((5, 4)),
             dma((5, 2)),
             dma((5, 2)),
             dma((6,)),

time: 34.7 us -> 34 us (0.980)
  Pallas kernels: 34 us -> 33.3 us
    pallas_call x1, Pallas kernels: 33.2 us -> 32.5 us  [local(): pl.pallas_call(kernel, out_shape=(pltpu.VMEM((2, 32, 1024), F32), pltpu.V...]
where the time goes in v3:
time: 34 us; the launch traced here: 33.9 us
  Pallas kernels  33.3 us (98%)
  between operations  0.64 us (2%)
    pallas_call x1, Pallas kernels, local(): pl.pallas_call(kernel, out_shape=(pltpu.VMEM((2, 32, 1024), F32), pltpu.V...  32.5 us
    pallas_call x1, Pallas kernels, local(): pl.pallas_call(store, out_shape=(jax.ShapeDtypeStruct((2, 32, 1024), F32)...  0.72 us

profile of v3, /device:TPU:1, one launch (start us, length us, event | category | flops | bytes accessed | tf_op | source)
XLA Modules:
  0.0 33.9 jit_solution(3753620137313845637)
XLA Ops:
  0.6 32.5 %shard_map.86 = (f32[2,32,1024]{2,1,0:T(8,128)S(1)}, f32[2,4,1024]{2,1,0:T(4,128)S(1)}) custom-call(bf16[2,32,1024]{2,1,0:T(8,128)(2,1)} %res_hbm.1, bf16[2,32,1024]{2,1,0:T(8,128)(2,1)} %trav_hbm.1, s32[1,3,2,4]{3,2,1,0:T(2,128)} %bitcast.1, bf16[4,256,256]{2,1,0:T(8,128)(2,1)} %constant.8.clone.perm_hbm, ...), custom_call_target="tpu_custom_call" | custom-call | tf_op jit(solution)/shard_map/pallas_call | solution.py:548
  33.2 0.7 %shard_map.87 = (f32[2,32,1024]{2,1,0:T(8,128)}, f32[2,4,1024]{2,1,0:T(4,128)}) custom-call(f32[2,32,1024]{2,1,0:T(8,128)S(1)} %get-tuple-element.4.res_ref, f32[2,4,1024]{2,1,0:T(4,128)S(1)} %get-tuple-element.5.trav_ref), custom_call_target="tpu_custom_call" | custom-call | tf_op jit(solution)/shard_map/pallas_call | solution.py:597

commit v4 on v3

--- a/solution.py
+++ b/solution.py
@@ -42,10 +42,10 @@
     high = both.astype(jnp.bfloat16)
     low = (both - high.astype(np.float32)).astype(jnp.bfloat16)
     weights = np.stack([high, low], axis=2)
-    small = np.kron(np.eye(2), sine).astype(np.float32)
+    small = np.kron(np.eye(4), sine).astype(np.float32)
     small_high = small.astype(jnp.bfloat16)
     small_low = (small - small_high.astype(np.float32)).astype(jnp.bfloat16)
-    rows = np.concatenate([small_high, small_high, small_low, small_low], axis=1)
+    rows = np.concatenate([small_high, small_high, small_low], axis=1)
     return (
         perms.astype(jnp.bfloat16),
         weights,
@@ -107,7 +107,7 @@
     out = []
     for p in range(4):
         high, low = split(g[p])
-        out.append(dot(rows, jnp.concatenate([high, low, high, low], axis=0)))
+        out.append(dot(rows, jnp.concatenate([high, low, high], axis=0)))
     return out
 
 
@@ -243,18 +243,12 @@
 
     pl.semaphore_wait(barrier, 7)
 
-    hops = []
-    for near in range(2):
-        slot = near * 2 + core
-        hop = remote(
-            mine.at[y],
-            tbuf.at[slot, y],
-            z_send.at[near],
-            t_recv.at[slot, y],
-            (around(first + 3), grp) if near else (around(first + 5), across_z),
-        )
-        hop.start()
-        hops.append(hop)
+    far = remote(mine.at[y], tbuf.at[core, y], z_send.at[0], t_recv.at[core, y], (around(first + 5), across_z))
+    far.start()
+
+    def near(c):
+        src = mine.at[y] if c else tbuf.at[4, y]
+        return remote(src, tbuf.at[2 + c, y], z_send.at[1 + c], t_recv.at[2 + c, y], (around(first + 3), grp))
 
     def to_partner(slot, src):
         return remote(src, tbuf.at[slot], x_send.at[slot], x_recv.at[slot], partner)
@@ -269,8 +263,7 @@
             ubuf[r, rb] = h[r * 32 : (r + 1) * 32]
     res_acc[...] = jnp.zeros_like(res_acc)
 
-    for e in (0, 4):
-        other[e] = jnp.zeros((4, 2, 2, 8, 512), F32)
+    other[0] = jnp.zeros((4, 2, 2, 8, 512), F32)
 
     def quarter(slot, q):
         return remote(mine.at[q], tbuf.at[slot, q], z_send.at[0], t_recv.at[slot, q], partner)
@@ -314,26 +307,27 @@
             ]
         return copies
 
-    def solve(i):
-        s = lax.rem(3 - i + core, 4)
-        pick = [[pair_ref[0, e, p, s] for e in range(3)] for p in range(2)]
-        both = []
-        for t in range(2):
-            wide = tbuf[i, :, t].astype(F32).reshape(4, 2, 8, 512)
-            both.append([wide[:, rb].reshape(32, 512) for rb in range(2)])
-        u, w = [], []
-        for p in range(2):
-            u.append([ubuf[pick[p][0], rb] for rb in range(2)])
-            second = pick[p][1] == 1
-            w.append([jnp.where(second, both[1][rb], both[0][rb]) for rb in range(2)])
-        d = [jnp.concatenate([u[p][rb] * w[p][rb] for p in range(2)], axis=0) for rb in range(2)]
+    def solve(slots):
+        u, w, factors = [], [], []
+        for slot in slots:
+            s = lax.rem(3 - slot + core, 4)
+            both = []
+            for t in range(2):
+                wide = tbuf[slot, :, t].astype(F32).reshape(4, 2, 8, 512)
+                both.append([wide[:, rb].reshape(32, 512) for rb in range(2)])
+            for p in range(2):
+                r, t, active = (pair_ref[0, e, p, s] for e in range(3))
+                u.append([ubuf[r, rb] for rb in range(2)])
+                w.append([jnp.where(t == 1, both[1][rb], both[0][rb]) for rb in range(2)])
+                factors.append([[jnp.where(e == j, active, 0).astype(F32) for j in range(2)] for e in (r, t)])
+        d = [jnp.concatenate([u[f][rb] * w[f][rb] for f in range(4)], axis=0) for rb in range(2)]
         g = []
         for e in (d[0] + d[1], d[0] - d[1]):
             g += [e[:, :256] + e[:, 256:], e[:, :256] - e[:, 256:]]
         rows = rows_ref[...]
         g = along_rows(plane(g, weight_ref, 0), rows)
         g = [
-            (m.reshape(2, 32, 256) * scale_ref[p][None]).reshape(64, 256)
+            (m.reshape(4, 32, 256) * scale_ref[p][None]).reshape(128, 256)
             for p, m in enumerate(g)
         ]
         g = plane(along_rows(g, rows), weight_ref, 1)
@@ -343,17 +337,17 @@
             (g[0] - g[2], g[1] - g[3]),
         ):
             pot.append(jnp.concatenate([e + o, e - o], axis=1))
-
-        def factor(p, e, value):
-            return jnp.where(pick[p][e] == value, pick[p][2], 0).astype(F32)
-
         for rb in range(2):
-            v = [pot[rb][p * 32 : (p + 1) * 32] for p in range(2)]
-            vw = [v[p] * w[p][rb] for p in range(2)]
-            vu = [v[p] * u[p][rb] for p in range(2)]
+            v = [pot[rb][f * 32 : (f + 1) * 32] for f in range(4)]
+            vw = [v[f] * w[f][rb] for f in range(4)]
+            vu = [v[f] * u[f][rb] for f in range(4)]
             for j in range(2):
-                res_acc[j, rb] += vw[0] * factor(0, 0, j) + vw[1] * factor(1, 0, j)
-                terms[i, :, j, rb] = (vu[0] * factor(0, 1, j) + vu[1] * factor(1, 1, j)).reshape(4, 8, 512)
+                ours = [vw[f] * factors[f][0][j] for f in range(4)]
+                res_acc[j, rb] += (ours[0] + ours[1]) + (ours[2] + ours[3])
+                for k, slot in enumerate(slots):
+                    f = 2 * k
+                    theirs = vu[f] * factors[f][1][j] + vu[f + 1] * factors[f + 1][1][j]
+                    terms[slot, :, j, rb] = theirs.reshape(4, 8, 512)
 
     def one_row(tiles):
         top = jnp.max(peak(tiles), axis=0, keepdims=True)
@@ -412,63 +406,74 @@
         for copy in h_copies(e):
             copy.start()
 
-    def first_order(i):
-        return (1 - i // 2) * (1 - i) + i // 2 * i
-
-    def spread_slots(slots):
-        for slot in slots:
-            for d in range(1, 4):
-                quarter(slot, y_peer(d)).wait_recv()
-            to_partner(slot, tbuf.at[slot]).start()
+    def relay(slot):
+        quarter(slot, y).wait_recv()
+        for d in range(1, 4):
+            forward(slot, d).start()
+
+    def spread_slot(slot):
+        for d in range(1, 4):
+            quarter(slot, y_peer(d)).wait_recv()
+        to_partner(slot, tbuf.at[slot]).start()
 
     def step(i, carry):
-        slot = (1 - core) * first_order(i) + core * (i + 4 * (1 - (i + 3) // 4))
+        @pl.when(jnp.logical_and(core == 1, i == 0))
+        def _():
+            to_partner(4, mine).wait_recv()
+            for c in range(2):
+                near(c).start()
+            relay(1)
+            relay(0)
+            spread_slot(1)
+            relay(3)
+            relay(2)
+            spread_slot(0)
 
         @pl.when(jnp.logical_and(core == 1, i == 1))
         def _():
-            for s in (1, 0, 3, 2):
-                quarter(s, y).wait_recv()
-                for d in range(1, 4):
-                    forward(s, d).start()
-            spread_slots((1, 0))
-
-        @pl.when(jnp.logical_and(core == 1, i == 2))
-        def _():
-            spread_slots((2, 3))
-
-        takes = jnp.logical_or(core == 0, i == 0)
-
-        @pl.when(takes)
-        def _():
-            to_partner(slot, mine).wait_recv()
-
-        solve(slot)
-
-        @pl.when(jnp.logical_not(takes))
-        def _():
-            to_other(slot).start()
-
-        @pl.when(jnp.logical_and(core == 0, slot > 0))
-        def _():
-            to_other(slot).wait_recv()
-
-        @pl.when(takes)
-        def _():
-            over_y(slot, terms[slot] + other[slot])
+            spread_slot(2)
+            spread_slot(3)
+
+        @pl.when(core == 0)
+        def _():
+            for k in range(2):
+                to_partner(2 * i + k, mine).wait_recv()
+
+        solve((i * 2 + (1 - i) * (1 + 3 * core), i * 3 + (1 - i) * core))
+
+        @pl.when(core == 0)
+        def _():
+            def combine(k, inner):
+                slot = 2 * i + k
+
+                @pl.when(slot > 0)
+                def _():
+                    to_other(slot).wait_recv()
+
+                over_y(slot, terms[slot] + other[slot])
+                return inner
+
+            lax.fori_loop(0, 2, combine, 0)
+
+        @pl.when(jnp.logical_and(core == 1, i == 0))
+        def _():
+            to_other(1).start()
+            over_y(4, terms[4])
+
+        @pl.when(jnp.logical_and(core == 1, i == 1))
+        def _():
+            to_other(2).start()
+            to_other(3).start()
 
         return carry
 
-    lax.fori_loop(0, 4, step, 0)
+    lax.fori_loop(0, 2, step, 0)
 
     for r in range(2):
         res_out[r] = restored([res_acc[r, rb] for rb in range(2)], perm_ref)
 
-    def entry_at(j):
-        later = (j + 4) // 5
-        return 4 * (1 - later) + later * first_order(j - later)
-
     def send_home(j, carry):
-        homeward(entry_at(j))
+        homeward(lax.rem(j + 4, 5))
         return carry
 
     @pl.when(core == 1)
@@ -500,8 +505,7 @@
 
     trav_out[...] = restored([total[rb] for rb in range(2)], perm_ref).reshape(2, 4, 1024)
 
-    for near in range(2):
-        hops[near].wait_send()
+    far.wait_send()
     for d in range(1, 4):
         for copy in y_copies(4 * core, d):
             copy.wait_send()
@@ -518,6 +522,8 @@
 
     @pl.when(core == 1)
     def _():
+        for c in range(2):
+            near(c).wait_send()
         for slot in range(4):
             for d in range(1, 4):
                 forward(slot, d).wait_send()
@@ -556,7 +562,7 @@
             pltpu.SMEM((1, 3, 2, 4), jnp.int32),
             pltpu.VMEM((4, 256, 256), BF16),
             pltpu.VMEM((2, 4, 2, 256, 256), BF16),
-            pltpu.VMEM((64, 256), BF16),
+            pltpu.VMEM((128, 384), BF16),
             pltpu.VMEM((4, 32, 256), F32),
             dma((7,)),
             pltpu.VMEM((4, 2, 16, 512), BF16),
@@ -574,7 +580,7 @@
             pltpu.VMEM((6, 16, 512), I16),
             pltpu.VMEM((6, 8, 128), F32),
             pltpu.VMEM((2, 8, 512), F32),
-            dma((2,)),
+            dma((3,)),
             dma((4, 3)),
             dma((4, 4)),
             dma((5,)),

time: 34 us -> 34.2 us (level)
  no operation moved by 1% of the time
where the time goes in v4:
time: 34.2 us; the launch traced here: 34 us
  Pallas kernels  33.4 us (98%)
  between operations  0.64 us (2%)
    pallas_call x1, Pallas kernels, local(): pl.pallas_call(kernel, out_shape=(pltpu.VMEM((2, 32, 1024), F32), pltpu.V...  32.7 us
    pallas_call x1, Pallas kernels, local(): pl.pallas_call(store, out_shape=(jax.ShapeDtypeStruct((2, 32, 1024), F32)...  0.72 us

profile of v4, /device:TPU:1, one launch (start us, length us, event | category | flops | bytes accessed | tf_op | source)
XLA Modules:
  0.0 34.0 jit_solution(13575914680061174214)
XLA Ops:
  0.6 32.7 %shard_map.86 = (f32[2,32,1024]{2,1,0:T(8,128)S(1)}, f32[2,4,1024]{2,1,0:T(4,128)S(1)}) custom-call(bf16[2,32,1024]{2,1,0:T(8,128)(2,1)} %res_hbm.1, bf16[2,32,1024]{2,1,0:T(8,128)(2,1)} %trav_hbm.1, s32[1,3,2,4]{3,2,1,0:T(2,128)} %bitcast.1, bf16[4,256,256]{2,1,0:T(8,128)(2,1)} %constant.8.clone.perm_hbm, ...), custom_call_target="tpu_custom_call" | custom-call | tf_op jit(solution)/shard_map/pallas_call | solution.py:554
  33.3 0.7 %shard_map.87 = (f32[2,32,1024]{2,1,0:T(8,128)}, f32[2,4,1024]{2,1,0:T(4,128)}) custom-call(f32[2,32,1024]{2,1,0:T(8,128)S(1)} %get-tuple-element.4.res_ref, f32[2,4,1024]{2,1,0:T(4,128)S(1)} %get-tuple-element.5.trav_ref), custom_call_target="tpu_custom_call" | custom-call | tf_op jit(solution)/shard_map/pallas_call | solution.py:603

commit v5 on v4

--- a/solution.py
+++ b/solution.py
@@ -45,11 +45,10 @@
     small = np.kron(np.eye(4), sine).astype(np.float32)
     small_high = small.astype(jnp.bfloat16)
     small_low = (small - small_high.astype(np.float32)).astype(jnp.bfloat16)
-    rows = np.concatenate([small_high, small_high, small_low], axis=1)
+    rows = np.concatenate([np.concatenate([small_high, small_low], axis=1), np.zeros((128, 256), jnp.bfloat16)])
     return (
         perms.astype(jnp.bfloat16),
-        weights,
-        rows,
+        np.concatenate([weights.reshape(16, 256, 256), rows[None]]),
         np.stack(scales).astype(np.float32),
     )
 
@@ -98,8 +97,8 @@
     for p in range(4):
         high, low = split(g[p])
         rows = high.shape[0]
-        a = dot(jnp.concatenate([high, low], axis=0), weight_ref[way, p, 0])
-        out.append(a[:rows] + a[rows:] + dot(high, weight_ref[way, p, 1]))
+        a = dot(jnp.concatenate([high, low], axis=0), weight_ref[way * 8 + p * 2])
+        out.append(a[:rows] + a[rows:] + dot(high, weight_ref[way * 8 + p * 2 + 1]))
     return out
 
 
@@ -139,7 +138,6 @@
     pair_hbm,
     perm_hbm,
     weight_hbm,
-    rows_hbm,
     scale_hbm,
     res_out,
     trav_out,
@@ -148,7 +146,6 @@
     pair_ref,
     perm_ref,
     weight_ref,
-    rows_ref,
     scale_ref,
     load_sem,
     mine,
@@ -159,6 +156,7 @@
     other,
     ycode,
     yscale,
+    ysent,
     yget,
     ygets,
     hcode,
@@ -167,8 +165,9 @@
     hgets,
     total,
     z_send,
+    z_recv,
     f_send,
-    t_recv,
+    f_recv,
     x_send,
     x_recv,
     c_send,
@@ -201,6 +200,12 @@
             src_ref=src, dst_ref=dst, send_sem=send, recv_sem=recv, device_id=to, device_id_type=MESH
         )
 
+    def came(ref, sem):
+        remote(ref, ref, sem, sem, partner).wait_recv()
+
+    def left(ref, sem):
+        remote(ref, ref, sem, sem, partner).wait_send()
+
     loads = [
         pltpu.make_async_copy(src, dst, load_sem.at[j])
         for j, (src, dst) in enumerate(
@@ -209,7 +214,6 @@
                 (perm_hbm, perm_ref),
                 (res_hbm, res_in),
                 (pair_hbm, pair_ref),
-                (rows_hbm, rows_ref),
                 (scale_hbm, scale_ref),
                 (weight_hbm, weight_ref),
             )
@@ -243,15 +247,15 @@
 
     pl.semaphore_wait(barrier, 7)
 
-    far = remote(mine.at[y], tbuf.at[core, y], z_send.at[0], t_recv.at[core, y], (around(first + 5), across_z))
+    far = remote(mine.at[y], tbuf.at[core, y], z_send, z_recv.at[core], (around(first + 5), across_z))
     far.start()
 
     def near(c):
         src = mine.at[y] if c else tbuf.at[4, y]
-        return remote(src, tbuf.at[2 + c, y], z_send.at[1 + c], t_recv.at[2 + c, y], (around(first + 3), grp))
+        return remote(src, tbuf.at[2 + c, y], z_send, z_recv.at[2 + c], (around(first + 3), grp))
 
     def to_partner(slot, src):
-        return remote(src, tbuf.at[slot], x_send.at[slot], x_recv.at[slot], partner)
+        return remote(src, tbuf.at[slot], x_send, x_recv.at[slot // 2 % 2], partner)
 
     @pl.when(core == 0)
     def _():
@@ -265,15 +269,12 @@
 
     other[0] = jnp.zeros((4, 2, 2, 8, 512), F32)
 
-    def quarter(slot, q):
-        return remote(mine.at[q], tbuf.at[slot, q], z_send.at[0], t_recv.at[slot, q], partner)
-
     def forward(slot, d):
         return remote(
             tbuf.at[slot, y],
             tbuf.at[slot, y],
-            f_send.at[slot, d - 1],
-            t_recv.at[slot, y],
+            f_send,
+            f_recv.at[slot],
             (blk, y_peer(d) * 2 + lo),
         )
 
@@ -281,19 +282,13 @@
         load.wait()
 
     def to_other(slot):
-        return remote(terms.at[slot], other.at[slot], c_send.at[slot], c_recv.at[slot], partner)
+        return remote(terms.at[slot], other.at[slot], c_send, c_recv.at[slot // 2], partner)
 
     def y_copies(e, d):
         to = (first + 1, y_peer(d) * 2 + lo)
         return (
-            remote(ycode.at[e, y_peer(d)], yget.at[e, d], y_send.at[e, d], y_recv.at[e, d], to),
-            remote(
-                yscale.at[e, pl.ds(0, 1)],
-                ygets.at[e, d, pl.ds(0, 1)],
-                ys_send.at[e, d],
-                ys_recv.at[e, d],
-                to,
-            ),
+            remote(ycode.at[e, y_peer(d)], yget.at[e, d], y_send, y_recv.at[e], to),
+            remote(yscale.at[pl.ds(e, 1)], ygets.at[e, pl.ds(d, 1)], ys_send, ys_recv.at[e], to),
         )
 
     def h_copies(e):
@@ -302,8 +297,8 @@
         for z in range(2):
             to = (around(first - 4 + e), y * 2 + z)
             copies += [
-                remote(hcode.at[e, z], hget.at[at], h_send.at[e, z], h_recv.at[at], to),
-                remote(hscale.at[e, pl.ds(0, 1)], hgets.at[at, pl.ds(0, 1)], hs_send.at[e, z], hs_recv.at[at], to),
+                remote(hcode.at[e, z], hget.at[at], h_send, h_recv, to),
+                remote(hscale.at[pl.ds(e, 1)], hgets.at[pl.ds(at, 1)], hs_send, hs_recv, to),
             ]
         return copies
 
@@ -324,7 +319,8 @@
         g = []
         for e in (d[0] + d[1], d[0] - d[1]):
             g += [e[:, :256] + e[:, 256:], e[:, :256] - e[:, 256:]]
-        rows = rows_ref[...]
+        high, low = weight_ref[16, :128, :128], weight_ref[16, :128, 128:]
+        rows = jnp.concatenate([high, high, low], axis=1)
         g = along_rows(plane(g, weight_ref, 0), rows)
         g = [
             (m.reshape(4, 32, 256) * scale_ref[p][None]).reshape(128, 256)
@@ -356,7 +352,7 @@
     def over_y(e, value):
         parts = [(q, t, rb) for q in range(4) for t in range(2) for rb in range(2)]
         top, wide = one_row([x for at in parts for x in lane_tiles(value[at])])
-        yscale[e, pl.ds(0, 1)] = top * (1.0 / TOP)
+        yscale[pl.ds(e, 1)] = top * (1.0 / TOP)
         wide = spread(wide, 4)
         for q in range(4):
             for t in range(2):
@@ -373,7 +369,7 @@
         @pl.when(core == 1)
         def _():
             yget[4, 0] = ycode[4, y]
-            ygets[4, 0, pl.ds(0, 1)] = yscale[4, pl.ds(0, 1)]
+            ygets[4, pl.ds(0, 1)] = yscale[pl.ds(4, 1)]
 
     def widened(code_ref, scale_row):
         code = code_ref[...].astype(jnp.int32).astype(F32)
@@ -383,15 +379,18 @@
     def homeward(e):
         @pl.when(e < 4)
         def _():
-            for copy in y_copies(e, 0):
-                copy.wait_recv()
-
-        sums = [widened(yget.at[e, 0, t], ygets[e, 0, pl.ds(0, 1)]) for t in range(2)]
-        for d in range(1, 4):
-            for copy in y_copies(e, d):
-                copy.wait_recv()
+            came(yget.at[e], y_recv.at[e])
+            came(ygets.at[e, pl.ds(0, 4)], ys_recv.at[e])
+
+        @pl.when(e == 4)
+        def _():
+            came(yget.at[4, pl.ds(1, 3)], y_recv.at[4])
+            came(ygets.at[4, pl.ds(1, 3)], ys_recv.at[4])
+
+        sums = [[0.0, 0.0], [0.0, 0.0]]
+        for d in range(4):
             for t in range(2):
-                for rb, part in enumerate(widened(yget.at[e, d, t], ygets[e, d, pl.ds(0, 1)])):
+                for rb, part in enumerate(widened(yget.at[e, d, t], ygets[e, pl.ds(d, 1)])):
                     sums[t][rb] += part
         upper = lax.broadcasted_iota(jnp.int32, (8, 512), 0) < 4
         rows = [
@@ -399,7 +398,7 @@
             [jnp.where(upper, pltpu.roll(sums[0][rb], 4, 0), sums[1][rb]) for rb in range(2)],
         ]
         top, wide = one_row([x for z in range(2) for rb in range(2) for x in lane_tiles(rows[z][rb])])
-        hscale[e, pl.ds(0, 1)] = top * (1.0 / TOP)
+        hscale[pl.ds(e, 1)] = top * (1.0 / TOP)
         wide = spread(wide, 4)
         for z in range(2):
             hcode[e, z] = jnp.concatenate([coded(rows[z][rb], wide) for rb in range(2)], axis=0).astype(I16)
@@ -407,26 +406,23 @@
             copy.start()
 
     def relay(slot):
-        quarter(slot, y).wait_recv()
+        came(tbuf.at[slot, y], z_recv.at[slot])
         for d in range(1, 4):
             forward(slot, d).start()
 
     def spread_slot(slot):
-        for d in range(1, 4):
-            quarter(slot, y_peer(d)).wait_recv()
+        came(tbuf.at[slot, pl.ds(0, 3)], f_recv.at[slot])
         to_partner(slot, tbuf.at[slot]).start()
 
     def step(i, carry):
         @pl.when(jnp.logical_and(core == 1, i == 0))
         def _():
-            to_partner(4, mine).wait_recv()
+            came(tbuf.at[4], x_recv.at[0])
             for c in range(2):
                 near(c).start()
-            relay(1)
-            relay(0)
+            for slot in (1, 0, 3, 2):
+                relay(slot)
             spread_slot(1)
-            relay(3)
-            relay(2)
             spread_slot(0)
 
         @pl.when(jnp.logical_and(core == 1, i == 1))
@@ -436,8 +432,7 @@
 
         @pl.when(core == 0)
         def _():
-            for k in range(2):
-                to_partner(2 * i + k, mine).wait_recv()
+            came(tbuf.at[pl.ds(2 * i, 2)], x_recv.at[i])
 
         solve((i * 2 + (1 - i) * (1 + 3 * core), i * 3 + (1 - i) * core))
 
@@ -446,9 +441,13 @@
             def combine(k, inner):
                 slot = 2 * i + k
 
-                @pl.when(slot > 0)
+                @pl.when(slot == 1)
                 def _():
-                    to_other(slot).wait_recv()
+                    came(other.at[1], c_recv.at[0])
+
+                @pl.when(slot == 2)
+                def _():
+                    came(other.at[pl.ds(2, 2)], c_recv.at[1])
 
                 over_y(slot, terms[slot] + other[slot])
                 return inner
@@ -480,59 +479,46 @@
     def _():
         lax.fori_loop(0, 5, send_home, 0)
 
-    def from_home(at):
-        return (
-            remote(hcode.at[0, 0], hget.at[at], h_send.at[0, 0], h_recv.at[at], partner),
-            remote(hscale.at[0, pl.ds(0, 1)], hgets.at[at, pl.ds(0, 1)], hs_send.at[0, 0], hs_recv.at[at], partner),
-        )
-
     def take(at):
-        for rb, part in enumerate(widened(hget.at[at], hgets[at, pl.ds(0, 1)])):
+        for rb, part in enumerate(widened(hget.at[at], hgets[pl.ds(at, 1)])):
             total[rb] += part
 
     total[...] = jnp.zeros_like(total)
-    for at in range(2, 6):
-        for copy in from_home(at):
-            copy.wait_recv()
-        take(at)
+
+    @pl.when(core == 1)
+    def _():
+        came(hget.at[pl.ds(2, 4)], h_recv)
+        came(hgets.at[pl.ds(2, 4)], hs_recv)
 
     @pl.when(core == 0)
     def _():
+        came(hget, h_recv)
+        came(hgets.at[pl.ds(0, 6)], hs_recv)
         for at in range(2):
-            for copy in from_home(at):
-                copy.wait_recv()
             take(at)
 
+    for at in range(2, 6):
+        take(at)
+
     trav_out[...] = restored([total[rb] for rb in range(2)], perm_ref).reshape(2, 4, 1024)
-
-    far.wait_send()
-    for d in range(1, 4):
-        for copy in y_copies(4 * core, d):
-            copy.wait_send()
 
     @pl.when(core == 0)
     def _():
-        to_partner(4, mine).wait_send()
-        for e in range(4):
-            for d in range(4):
-                if e == 0 and d > 0:
-                    continue
-                for copy in y_copies(e, d):
-                    copy.wait_send()
+        left(mine.at[0], z_send)
+        left(mine, x_send)
+        left(ycode.at[pl.ds(0, 4)], y_send)
+        left(ysent, ys_send)
 
     @pl.when(core == 1)
     def _():
-        for c in range(2):
-            near(c).wait_send()
-        for slot in range(4):
-            for d in range(1, 4):
-                forward(slot, d).wait_send()
-            to_partner(slot, mine).wait_send()
-            if slot:
-                to_other(slot).wait_send()
-        for e in range(5):
-            for copy in h_copies(e):
-                copy.wait_send()
+        left(mine.at[pl.ds(0, 3)], z_send)
+        left(tbuf.at[pl.ds(0, 3)], f_send)
+        left(tbuf.at[pl.ds(0, 4)], x_send)
+        left(terms.at[pl.ds(1, 3)], c_send)
+        left(ycode.at[4, pl.ds(0, 3)], y_send)
+        left(ysent.at[pl.ds(0, 3)], ys_send)
+        left(hcode, h_send)
+        left(ysent.at[pl.ds(0, 10)], hs_send)
 
 
 def store(res_ref, trav_ref, res_out, trav_out, sem):
@@ -554,17 +540,16 @@
     done = pl.pallas_call(
         kernel,
         out_shape=(pltpu.VMEM((2, 32, 1024), F32), pltpu.VMEM((2, 4, 1024), F32)),
-        in_specs=[hbm] * 7,
+        in_specs=[hbm] * 6,
         out_specs=(vmem, vmem),
         scratch_shapes=[
             pltpu.VMEM((2, 32, 1024), BF16),
             pltpu.VMEM((2, 32, 1024), BF16),
             pltpu.SMEM((1, 3, 2, 4), jnp.int32),
             pltpu.VMEM((4, 256, 256), BF16),
-            pltpu.VMEM((2, 4, 2, 256, 256), BF16),
-            pltpu.VMEM((128, 384), BF16),
+            pltpu.VMEM((17, 256, 256), BF16),
             pltpu.VMEM((4, 32, 256), F32),
-            dma((7,)),
+            dma((6,)),
             pltpu.VMEM((4, 2, 16, 512), BF16),
             pltpu.VMEM((5, 4, 2, 16, 512), BF16),
             pltpu.VMEM((2, 2, 32, 512), F32),
@@ -572,29 +557,31 @@
             pltpu.VMEM((5, 4, 2, 2, 8, 512), F32),
             pltpu.VMEM((5, 4, 2, 2, 8, 512), F32),
             pltpu.VMEM((5, 4, 2, 16, 512), I16),
+            pltpu.VMEM((8, 128), F32),
+            pltpu.VMEM((16, 128), F32),
+            pltpu.VMEM((5, 4, 2, 16, 512), I16),
             pltpu.VMEM((5, 8, 128), F32),
-            pltpu.VMEM((5, 4, 2, 16, 512), I16),
-            pltpu.VMEM((5, 4, 8, 128), F32),
             pltpu.VMEM((5, 2, 16, 512), I16),
-            pltpu.VMEM((5, 8, 128), F32),
+            pltpu.VMEM((8, 128), F32),
             pltpu.VMEM((6, 16, 512), I16),
-            pltpu.VMEM((6, 8, 128), F32),
+            pltpu.VMEM((8, 128), F32),
             pltpu.VMEM((2, 8, 512), F32),
-            dma((3,)),
-            dma((4, 3)),
-            dma((4, 4)),
+            dma,
+            dma((4,)),
+            dma,
+            dma((4,)),
+            dma,
+            dma((2,)),
+            dma,
+            dma((2,)),
+            dma,
+            dma,
             dma((5,)),
             dma((5,)),
-            dma((4,)),
-            dma((4,)),
-            dma((5, 4)),
-            dma((5, 4)),
-            dma((5, 4)),
-            dma((5, 4)),
-            dma((5, 2)),
-            dma((5, 2)),
-            dma((6,)),
-            dma((6,)),
+            dma,
+            dma,
+            dma,
+            dma,
         ],
         compiler_params=pltpu.CompilerParams(
             collective_id=0, has_side_effects=True

time: 34.2 us -> 32 us (0.936)
  Pallas kernels: 33.4 us -> 31.2 us
    pallas_call x1, Pallas kernels: 32.7 us -> 30.5 us  [local(): pl.pallas_call(kernel, out_shape=(pltpu.VMEM((2, 32, 1024), F32), pltpu.V...]
where the time goes in v5:
time: 32 us; the launch traced here: 31.9 us
  Pallas kernels  31.2 us (98%)
  between operations  0.64 us (2%)
    pallas_call x1, Pallas kernels, local(): pl.pallas_call(kernel, out_shape=(pltpu.VMEM((2, 32, 1024), F32), pltpu.V...  30.5 us
    pallas_call x1, Pallas kernels, local(): pl.pallas_call(store, out_shape=(jax.ShapeDtypeStruct((2, 32, 1024), F32)...  0.72 us

profile of v5, /device:TPU:1, one launch (start us, length us, event | category | flops | bytes accessed | tf_op | source)
XLA Modules:
  0.0 31.9 jit_solution(15315786551619441181)
XLA Ops:
  0.6 30.5 %shard_map.77 = (f32[2,32,1024]{2,1,0:T(8,128)S(1)}, f32[2,4,1024]{2,1,0:T(4,128)S(1)}) custom-call(bf16[2,32,1024]{2,1,0:T(8,128)(2,1)} %res_hbm.1, bf16[2,32,1024]{2,1,0:T(8,128)(2,1)} %trav_hbm.1, s32[1,3,2,4]{3,2,1,0:T(2,128)} %bitcast.1, bf16[4,256,256]{2,1,0:T(8,128)(2,1)} %constant.6.clone.perm_hbm, bf16[17,256,256]{2,1,0:T(8,128)(2,1)} %constant.7.clone.weight_hbm, ...), custom_call_target="tpu_custom_call" | custom-call | tf_op jit(solution)/shard_map/pallas_call | solution.py:540
  31.1 0.7 %shard_map.78 = (f32[2,32,1024]{2,1,0:T(8,128)}, f32[2,4,1024]{2,1,0:T(4,128)}) custom-call(f32[2,32,1024]{2,1,0:T(8,128)S(1)} %get-tuple-element.4.res_ref, f32[2,4,1024]{2,1,0:T(4,128)S(1)} %get-tuple-element.5.trav_ref), custom_call_target="tpu_custom_call" | custom-call | tf_op jit(solution)/shard_map/pallas_call | solution.py:590

commit v6 on v5

--- a/solution.py
+++ b/solution.py
@@ -45,7 +45,7 @@
     small = np.kron(np.eye(4), sine).astype(np.float32)
     small_high = small.astype(jnp.bfloat16)
     small_low = (small - small_high.astype(np.float32)).astype(jnp.bfloat16)
-    rows = np.concatenate([np.concatenate([small_high, small_low], axis=1), np.zeros((128, 256), jnp.bfloat16)])
+    rows = np.block([[small_high, small_high], [small_low, small_low]])
     return (
         perms.astype(jnp.bfloat16),
         np.concatenate([weights.reshape(16, 256, 256), rows[None]]),
@@ -105,8 +105,9 @@
 def along_rows(g, rows):
     out = []
     for p in range(4):
-        high, low = split(g[p])
-        out.append(dot(rows, jnp.concatenate([high, low, high], axis=0)))
+        both = dot(rows, jnp.concatenate(split(g[p]), axis=0))
+        half = both.shape[0] // 2
+        out.append(both[:half] + both[half:])
     return out
 
 
@@ -282,7 +283,7 @@
         load.wait()
 
     def to_other(slot):
-        return remote(terms.at[slot], other.at[slot], c_send, c_recv.at[slot // 2], partner)
+        return remote(terms.at[slot], other.at[slot], c_send, c_recv.at[slot - 1], partner)
 
     def y_copies(e, d):
         to = (first + 1, y_peer(d) * 2 + lo)
@@ -319,8 +320,7 @@
         g = []
         for e in (d[0] + d[1], d[0] - d[1]):
             g += [e[:, :256] + e[:, 256:], e[:, :256] - e[:, 256:]]
-        high, low = weight_ref[16, :128, :128], weight_ref[16, :128, 128:]
-        rows = jnp.concatenate([high, high, low], axis=1)
+        rows = weight_ref[16]
         g = along_rows(plane(g, weight_ref, 0), rows)
         g = [
             (m.reshape(4, 32, 256) * scale_ref[p][None]).reshape(128, 256)
@@ -357,7 +357,7 @@
         for q in range(4):
             for t in range(2):
                 ycode[e, q, t] = jnp.concatenate([coded(value[q, t, rb], wide) for rb in range(2)], axis=0).astype(I16)
-        for d in range(1, 4):
+        for d in (2, 1, 3):
             for copy in y_copies(e, d):
                 copy.start()
 
@@ -407,7 +407,7 @@
 
     def relay(slot):
         came(tbuf.at[slot, y], z_recv.at[slot])
-        for d in range(1, 4):
+        for d in (2, 1, 3):
             forward(slot, d).start()
 
     def spread_slot(slot):
@@ -441,13 +441,9 @@
             def combine(k, inner):
                 slot = 2 * i + k
 
-                @pl.when(slot == 1)
+                @pl.when(slot > 0)
                 def _():
-                    came(other.at[1], c_recv.at[0])
-
-                @pl.when(slot == 2)
-                def _():
-                    came(other.at[pl.ds(2, 2)], c_recv.at[1])
+                    to_other(slot).wait_recv()
 
                 over_y(slot, terms[slot] + other[slot])
                 return inner
@@ -573,7 +569,7 @@
             dma,
             dma((2,)),
             dma,
-            dma((2,)),
+            dma((3,)),
             dma,
             dma,
             dma((5,)),

time: 32 us -> 31.4 us (0.981)
  Pallas kernels: 31.2 us -> 30.7 us
    pallas_call x1, Pallas kernels: 30.5 us -> 30 us  [local(): pl.pallas_call(kernel, out_shape=(pltpu.VMEM((2, 32, 1024), F32), pltpu.V...]
where the time goes in v6:
time: 31.4 us; the launch traced here: 31.3 us
  Pallas kernels  30.7 us (98%)
  between operations  0.64 us (2%)
    pallas_call x1, Pallas kernels, local(): pl.pallas_call(kernel, out_shape=(pltpu.VMEM((2, 32, 1024), F32), pltpu.V...  30 us
    pallas_call x1, Pallas kernels, local(): pl.pallas_call(store, out_shape=(jax.ShapeDtypeStruct((2, 32, 1024), F32)...  0.72 us

profile of v6, /device:TPU:1, one launch (start us, length us, event | category | flops | bytes accessed | tf_op | source)
XLA Modules:
  0.0 31.3 jit_solution(17067812879758458928)
XLA Ops:
  0.6 30.0 %shard_map.77 = (f32[2,32,1024]{2,1,0:T(8,128)S(1)}, f32[2,4,1024]{2,1,0:T(4,128)S(1)}) custom-call(bf16[2,32,1024]{2,1,0:T(8,128)(2,1)} %res_hbm.1, bf16[2,32,1024]{2,1,0:T(8,128)(2,1)} %trav_hbm.1, s32[1,3,2,4]{3,2,1,0:T(2,128)} %bitcast.1, bf16[4,256,256]{2,1,0:T(8,128)(2,1)} %constant.6.clone.perm_hbm, bf16[17,256,256]{2,1,0:T(8,128)(2,1)} %constant.7.clone.weight_hbm, ...), custom_call_target="tpu_custom_call" | custom-call | tf_op jit(solution)/shard_map/pallas_call | solution.py:536
  30.6 0.7 %shard_map.78 = (f32[2,32,1024]{2,1,0:T(8,128)}, f32[2,4,1024]{2,1,0:T(4,128)}) custom-call(f32[2,32,1024]{2,1,0:T(8,128)S(1)} %get-tuple-element.4.res_ref, f32[2,4,1024]{2,1,0:T(4,128)S(1)} %get-tuple-element.5.trav_ref), custom_call_target="tpu_custom_call" | custom-call | tf_op jit(solution)/shard_map/pallas_call | solution.py:586

commit v7 on v6

--- a/solution.py
+++ b/solution.py
@@ -149,12 +149,12 @@
     weight_ref,
     scale_ref,
     load_sem,
-    mine,
     tbuf,
     ubuf,
+    table,
     res_acc,
+    res_got,
     terms,
-    other,
     ycode,
     yscale,
     ysent,
@@ -169,10 +169,12 @@
     z_recv,
     f_send,
     f_recv,
-    x_send,
-    x_recv,
-    c_send,
-    c_recv,
+    u_send,
+    u_recv,
+    p_send,
+    p_recv,
+    r_send,
+    r_recv,
     y_send,
     ys_send,
     y_recv,
@@ -228,67 +230,63 @@
     def arrive(to):
         pl.semaphore_signal(barrier, inc=1, device_id=to, device_id_type=MESH)
 
+    arrive((around(blk - 4), across_z))
+    arrive((around(blk - 2), grp))
+    for d in range(1, 4):
+        arrive((blk, y_peer(d) * 2 + lo))
+    arrive((blk, across_z))
     arrive(partner)
-    arrive((blk, across_z))
 
     @pl.when(core == 1)
     def _():
-        for c in range(2):
-            arrive((around(first - 4 + c), across_z))
-            arrive((around(first - 2 + c), grp))
-            for d in range(1, 4):
-                arrive((first + c, y_peer(d) * 2 + lo))
+        for d in range(1, 4):
+            arrive((first, y_peer(d) * 2 + lo))
 
     loads[0].wait()
     loads[1].wait()
     own = [h.reshape(2, 4, 8, 512) for h in permuted(trav_in[...].reshape(64, 1024), perm_ref)]
     for q in range(4):
         for t in range(2):
-            mine[q, t] = jnp.concatenate([own[0][t, q], own[1][t, q]], axis=0).astype(BF16)
-
-    pl.semaphore_wait(barrier, 7)
-
-    far = remote(mine.at[y], tbuf.at[core, y], z_send, z_recv.at[core], (around(first + 5), across_z))
-    far.start()
-
-    def near(c):
-        src = mine.at[y] if c else tbuf.at[4, y]
-        return remote(src, tbuf.at[2 + c, y], z_send, z_recv.at[2 + c], (around(first + 3), grp))
-
-    def to_partner(slot, src):
-        return remote(src, tbuf.at[slot], x_send, x_recv.at[slot // 2 % 2], partner)
-
-    @pl.when(core == 0)
-    def _():
-        to_partner(4, mine).start()
+            tbuf[16 + q, t] = jnp.concatenate([own[0][t, q], own[1][t, q]], axis=0).astype(BF16)
+
+    pl.semaphore_wait(barrier, 7 + 3 * (1 - core))
+
+    def onward(near):
+        to = (around(blk + 2), grp) if near else (around(blk + 4), across_z)
+        return remote(tbuf.at[16 + y], tbuf.at[4 * (2 * near + core) + y], z_send, z_recv.at[near], to)
+
+    onward(0).start()
 
     loads[2].wait()
     for rb, h in enumerate(permuted(res_in[...].reshape(64, 1024), perm_ref)):
         for r in range(2):
-            ubuf[r, rb] = h[r * 32 : (r + 1) * 32]
+            ubuf[0, r, rb] = h[r * 32 : (r + 1) * 32].reshape(4, 8, 512)
+    loads[3].wait()
+    for s in range(4):
+        for e in range(3):
+            for p in range(2):
+                table[0, s, 2 * e + p] = jnp.full((8, 128), pair_ref[0, e, p, s].astype(F32))
+    shares = [
+        remote(ubuf.at[0], ubuf.at[1], u_send, u_recv, partner),
+        remote(table.at[0], table.at[1], p_send, p_recv, partner),
+    ]
+    for share in shares:
+        share.start()
     res_acc[...] = jnp.zeros_like(res_acc)
-
-    other[0] = jnp.zeros((4, 2, 2, 8, 512), F32)
-
-    def forward(slot, d):
-        return remote(
-            tbuf.at[slot, y],
-            tbuf.at[slot, y],
-            f_send,
-            f_recv.at[slot],
-            (blk, y_peer(d) * 2 + lo),
-        )
-
-    for load in loads[3:]:
+    for load in loads[4:]:
         load.wait()
-
-    def to_other(slot):
-        return remote(terms.at[slot], other.at[slot], c_send, c_recv.at[slot - 1], partner)
+    for share in shares:
+        share.wait_recv()
+    onward(1).start()
+
+    def forward(near, d):
+        at = 4 * (2 * near + core) + y
+        return remote(tbuf.at[at], tbuf.at[at], f_send, f_recv.at[near], (blk, y_peer(d) * 2 + lo))
 
     def y_copies(e, d):
         to = (first + 1, y_peer(d) * 2 + lo)
         return (
-            remote(ycode.at[e, y_peer(d)], yget.at[e, d], y_send, y_recv.at[e], to),
+            remote(ycode.at[4 * e + y_peer(d)], yget.at[e, d], y_send, y_recv.at[e], to),
             remote(yscale.at[pl.ds(e, 1)], ygets.at[e, pl.ds(d, 1)], ys_send, ys_recv.at[e], to),
         )
 
@@ -305,18 +303,21 @@
 
     def solve(slots):
         u, w, factors = [], [], []
-        for slot in slots:
-            s = lax.rem(3 - slot + core, 4)
+        for owner, slot in enumerate(slots):
+            s = (core if owner == 0 else 1 - core) + 3 - slot
             both = []
             for t in range(2):
-                wide = tbuf[slot, :, t].astype(F32).reshape(4, 2, 8, 512)
-                both.append([wide[:, rb].reshape(32, 512) for rb in range(2)])
+                wide = tbuf[pl.ds(4 * slot, 4), t].astype(F32).reshape(4, 2, 8, 512)
+                both.append([wide[:, rb] for rb in range(2)])
             for p in range(2):
-                r, t, active = (pair_ref[0, e, p, s] for e in range(3))
-                u.append([ubuf[r, rb] for rb in range(2)])
-                w.append([jnp.where(t == 1, both[1][rb], both[0][rb]) for rb in range(2)])
-                factors.append([[jnp.where(e == j, active, 0).astype(F32) for j in range(2)] for e in (r, t)])
-        d = [jnp.concatenate([u[f][rb] * w[f][rb] for f in range(4)], axis=0) for rb in range(2)]
+                r, t, active = (spread(table[owner, s, 2 * e + p], 4)[None] for e in range(3))
+                u.append([jnp.where(r > 0.5, ubuf[owner, 1, rb], ubuf[owner, 0, rb]) for rb in range(2)])
+                w.append([jnp.where(t > 0.5, both[1][rb], both[0][rb]) for rb in range(2)])
+                factors.append([[active - active * e, active * e] for e in (r, t)])
+        d = [
+            jnp.concatenate([(u[f][rb] * w[f][rb]).reshape(32, 512) for f in range(4)], axis=0)
+            for rb in range(2)
+        ]
         g = []
         for e in (d[0] + d[1], d[0] - d[1]):
             g += [e[:, :256] + e[:, 256:], e[:, :256] - e[:, 256:]]
@@ -334,16 +335,14 @@
         ):
             pot.append(jnp.concatenate([e + o, e - o], axis=1))
         for rb in range(2):
-            v = [pot[rb][f * 32 : (f + 1) * 32] for f in range(4)]
-            vw = [v[f] * w[f][rb] for f in range(4)]
-            vu = [v[f] * u[f][rb] for f in range(4)]
-            for j in range(2):
-                ours = [vw[f] * factors[f][0][j] for f in range(4)]
-                res_acc[j, rb] += (ours[0] + ours[1]) + (ours[2] + ours[3])
-                for k, slot in enumerate(slots):
-                    f = 2 * k
-                    theirs = vu[f] * factors[f][1][j] + vu[f + 1] * factors[f + 1][1][j]
-                    terms[slot, :, j, rb] = theirs.reshape(4, 8, 512)
+            v = [pot[rb][f * 32 : (f + 1) * 32].reshape(4, 8, 512) for f in range(4)]
+            for owner in range(2):
+                f, f1 = 2 * owner, 2 * owner + 1
+                vw, vw1 = v[f] * w[f][rb], v[f1] * w[f1][rb]
+                vu, vu1 = v[f] * u[f][rb], v[f1] * u[f1][rb]
+                for j in range(2):
+                    res_acc[owner, j, rb] += vw * factors[f][0][j] + vw1 * factors[f1][0][j]
+                    terms[owner, :, j, rb] = vu * factors[f][1][j] + vu1 * factors[f1][1][j]
 
     def one_row(tiles):
         top = jnp.max(peak(tiles), axis=0, keepdims=True)
@@ -356,7 +355,7 @@
         wide = spread(wide, 4)
         for q in range(4):
             for t in range(2):
-                ycode[e, q, t] = jnp.concatenate([coded(value[q, t, rb], wide) for rb in range(2)], axis=0).astype(I16)
+                ycode[4 * e + q, t] = jnp.concatenate([coded(value[q, t, rb], wide) for rb in range(2)], axis=0).astype(I16)
         for d in (2, 1, 3):
             for copy in y_copies(e, d):
                 copy.start()
@@ -368,8 +367,8 @@
 
         @pl.when(core == 1)
         def _():
-            yget[4, 0] = ycode[4, y]
-            ygets[4, pl.ds(0, 1)] = yscale[pl.ds(4, 1)]
+            yget[e, 0] = ycode[4 * e + y]
+            ygets[e, pl.ds(0, 1)] = yscale[pl.ds(e, 1)]
 
     def widened(code_ref, scale_row):
         code = code_ref[...].astype(jnp.int32).astype(F32)
@@ -377,15 +376,15 @@
         return [code[rb * 8 : (rb + 1) * 8] * scale for rb in range(2)]
 
     def homeward(e):
-        @pl.when(e < 4)
+        @pl.when(lax.rem(e, 2) == 0)
         def _():
             came(yget.at[e], y_recv.at[e])
             came(ygets.at[e, pl.ds(0, 4)], ys_recv.at[e])
 
-        @pl.when(e == 4)
+        @pl.when(lax.rem(e, 2) == 1)
         def _():
-            came(yget.at[4, pl.ds(1, 3)], y_recv.at[4])
-            came(ygets.at[4, pl.ds(1, 3)], ys_recv.at[4])
+            came(yget.at[e, pl.ds(1, 3)], y_recv.at[e])
+            came(ygets.at[e, pl.ds(1, 3)], ys_recv.at[e])
 
         sums = [[0.0, 0.0], [0.0, 0.0]]
         for d in range(4):
@@ -405,75 +404,47 @@
         for copy in h_copies(e):
             copy.start()
 
-    def relay(slot):
-        came(tbuf.at[slot, y], z_recv.at[slot])
-        for d in (2, 1, 3):
-            forward(slot, d).start()
-
-    def spread_slot(slot):
-        came(tbuf.at[slot, pl.ds(0, 3)], f_recv.at[slot])
-        to_partner(slot, tbuf.at[slot]).start()
-
     def step(i, carry):
-        @pl.when(jnp.logical_and(core == 1, i == 0))
+        @pl.when(i == 0)
         def _():
-            came(tbuf.at[4], x_recv.at[0])
-            for c in range(2):
-                near(c).start()
-            for slot in (1, 0, 3, 2):
-                relay(slot)
-            spread_slot(1)
-            spread_slot(0)
-
-        @pl.when(jnp.logical_and(core == 1, i == 1))
+            for near in range(2):
+                came(tbuf.at[4 * (2 * near + core) + y], z_recv.at[near])
+                for d in (2, 1, 3):
+                    forward(near, d).start()
+
+        came(tbuf.at[pl.ds(0, 3)], f_recv.at[i])
+        slot = 2 * i + core
+        apart = (1 - core) * (1 - i)
+        solve((slot, slot + 4 * apart))
+
+        @pl.when(apart == 0)
         def _():
-            spread_slot(2)
-            spread_slot(3)
-
-        @pl.when(core == 0)
-        def _():
-            came(tbuf.at[pl.ds(2 * i, 2)], x_recv.at[i])
-
-        solve((i * 2 + (1 - i) * (1 + 3 * core), i * 3 + (1 - i) * core))
-
-        @pl.when(core == 0)
-        def _():
-            def combine(k, inner):
-                slot = 2 * i + k
-
-                @pl.when(slot > 0)
-                def _():
-                    to_other(slot).wait_recv()
-
-                over_y(slot, terms[slot] + other[slot])
-                return inner
-
-            lax.fori_loop(0, 2, combine, 0)
-
-        @pl.when(jnp.logical_and(core == 1, i == 0))
-        def _():
-            to_other(1).start()
-            over_y(4, terms[4])
-
-        @pl.when(jnp.logical_and(core == 1, i == 1))
-        def _():
-            to_other(2).start()
-            to_other(3).start()
-
+            terms[0] += terms[1]
+
+        def send(k, inner):
+            over_y(slot + 4 * k, terms[k])
+            return inner
+
+        lax.fori_loop(0, 1 + apart, send, 0)
         return carry
 
     lax.fori_loop(0, 2, step, 0)
 
-    for r in range(2):
-        res_out[r] = restored([res_acc[r, rb] for rb in range(2)], perm_ref)
+    back = remote(res_acc.at[1], res_got, r_send, r_recv, partner)
+    back.start()
 
     def send_home(j, carry):
-        homeward(lax.rem(j + 4, 5))
+        even = (j + 3) // 5
+        homeward((1 - even) * (2 * j + 1) + even * lax.rem(4 * j + 4, 6))
         return carry
 
     @pl.when(core == 1)
     def _():
         lax.fori_loop(0, 5, send_home, 0)
+
+    back.wait_recv()
+    for r in range(2):
+        res_out[r] = restored([(res_acc[0, r, rb] + res_got[r, rb]).reshape(32, 512) for rb in range(2)], perm_ref)
 
     def take(at):
         for rb, part in enumerate(widened(hget.at[at], hgets[pl.ds(at, 1)])):
@@ -498,21 +469,21 @@
 
     trav_out[...] = restored([total[rb] for rb in range(2)], perm_ref).reshape(2, 4, 1024)
 
+    left(tbuf.at[pl.ds(0, 2)], z_send)
+    left(tbuf.at[pl.ds(0, 6)], f_send)
+    for share in shares:
+        share.wait_send()
+    back.wait_send()
+
     @pl.when(core == 0)
     def _():
-        left(mine.at[0], z_send)
-        left(mine, x_send)
-        left(ycode.at[pl.ds(0, 4)], y_send)
-        left(ysent, ys_send)
+        left(ycode.at[pl.ds(0, 12)], y_send)
+        left(ysent.at[pl.ds(0, 12)], ys_send)
 
     @pl.when(core == 1)
     def _():
-        left(mine.at[pl.ds(0, 3)], z_send)
-        left(tbuf.at[pl.ds(0, 3)], f_send)
-        left(tbuf.at[pl.ds(0, 4)], x_send)
-        left(terms.at[pl.ds(1, 3)], c_send)
-        left(ycode.at[4, pl.ds(0, 3)], y_send)
-        left(ysent.at[pl.ds(0, 3)], ys_send)
+        left(ycode.at[pl.ds(0, 6)], y_send)
+        left(ysent.at[pl.ds(0, 6)], ys_send)
         left(hcode, h_send)
         left(ysent.at[pl.ds(0, 10)], hs_send)
 
@@ -546,13 +517,13 @@
             pltpu.VMEM((17, 256, 256), BF16),
             pltpu.VMEM((4, 32, 256), F32),
             dma((6,)),
-            pltpu.VMEM((4, 2, 16, 512), BF16),
-            pltpu.VMEM((5, 4, 2, 16, 512), BF16),
-            pltpu.VMEM((2, 2, 32, 512), F32),
-            pltpu.VMEM((2, 2, 32, 512), F32),
-            pltpu.VMEM((5, 4, 2, 2, 8, 512), F32),
-            pltpu.VMEM((5, 4, 2, 2, 8, 512), F32),
-            pltpu.VMEM((5, 4, 2, 16, 512), I16),
+            pltpu.VMEM((20, 2, 16, 512), BF16),
+            pltpu.VMEM((2, 2, 2, 4, 8, 512), F32),
+            pltpu.VMEM((2, 4, 6, 8, 128), F32),
+            pltpu.VMEM((2, 2, 2, 4, 8, 512), F32),
+            pltpu.VMEM((2, 2, 4, 8, 512), F32),
+            pltpu.VMEM((2, 4, 2, 2, 8, 512), F32),
+            pltpu.VMEM((20, 2, 16, 512), I16),
             pltpu.VMEM((8, 128), F32),
             pltpu.VMEM((16, 128), F32),
             pltpu.VMEM((5, 4, 2, 16, 512), I16),
@@ -563,13 +534,15 @@
             pltpu.VMEM((8, 128), F32),
             pltpu.VMEM((2, 8, 512), F32),
             dma,
-            dma((4,)),
-            dma,
-            dma((4,)),
-            dma,
             dma((2,)),
             dma,
-            dma((3,)),
+            dma((2,)),
+            dma,
+            dma,
+            dma,
+            dma,
+            dma,
+            dma,
             dma,
             dma,
             dma((5,)),

time: 31.4 us -> 29.7 us (0.946)
  Pallas kernels: 30.7 us -> 29 us
    pallas_call x1, Pallas kernels: 30 us -> 28.3 us  [local(): pl.pallas_call(kernel, out_shape=(pltpu.VMEM((2, 32, 1024), F32), pltpu.V...]
where the time goes in v7:
time: 29.7 us; the launch traced here: 29.6 us
  Pallas kernels  29 us (98%)
  between operations  0.64 us (2%)
    pallas_call x1, Pallas kernels, local(): pl.pallas_call(kernel, out_shape=(pltpu.VMEM((2, 32, 1024), F32), pltpu.V...  28.3 us
    pallas_call x1, Pallas kernels, local(): pl.pallas_call(store, out_shape=(jax.ShapeDtypeStruct((2, 32, 1024), F32)...  0.72 us

profile of v7, /device:TPU:1, one launch (start us, length us, event | category | flops | bytes accessed | tf_op | source)
XLA Modules:
  0.0 29.6 jit_solution(1832287247223700479)
XLA Ops:
  0.6 28.3 %shard_map.77 = (f32[2,32,1024]{2,1,0:T(8,128)S(1)}, f32[2,4,1024]{2,1,0:T(4,128)S(1)}) custom-call(bf16[2,32,1024]{2,1,0:T(8,128)(2,1)} %res_hbm.1, bf16[2,32,1024]{2,1,0:T(8,128)(2,1)} %trav_hbm.1, s32[1,3,2,4]{3,2,1,0:T(2,128)} %bitcast.1, bf16[4,256,256]{2,1,0:T(8,128)(2,1)} %constant.6.clone.perm_hbm, bf16[17,256,256]{2,1,0:T(8,128)(2,1)} %constant.7.clone.weight_hbm, ...), custom_call_target="tpu_custom_call" | custom-call | tf_op jit(solution)/shard_map/pallas_call | solution.py:507
  28.9 0.7 %shard_map.78 = (f32[2,32,1024]{2,1,0:T(8,128)}, f32[2,4,1024]{2,1,0:T(4,128)}) custom-call(f32[2,32,1024]{2,1,0:T(8,128)S(1)} %get-tuple-element.4.res_ref, f32[2,4,1024]{2,1,0:T(4,128)S(1)} %get-tuple-element.5.trav_ref), custom_call_target="tpu_custom_call" | custom-call | tf_op jit(solution)/shard_map/pallas_call | solution.py:559

commit v8 on v7

--- a/solution.py
+++ b/solution.py
@@ -46,9 +46,11 @@
     small_high = small.astype(jnp.bfloat16)
     small_low = (small - small_high.astype(np.float32)).astype(jnp.bfloat16)
     rows = np.block([[small_high, small_high], [small_low, small_low]])
+    pair = np.zeros((256, 256), jnp.bfloat16)
+    pair[:128, :128] = np.block([[t[:64, :64]] * 2 for t in (small_high, small_low)])
     return (
         perms.astype(jnp.bfloat16),
-        np.concatenate([weights.reshape(16, 256, 256), rows[None]]),
+        np.concatenate([weights.reshape(16, 256, 256), rows[None], pair[None]]),
         np.stack(scales).astype(np.float32),
     )
 
@@ -169,6 +171,8 @@
     z_recv,
     f_send,
     f_recv,
+    w_send,
+    w_recv,
     u_send,
     u_recv,
     p_send,
@@ -256,6 +260,11 @@
         return remote(tbuf.at[16 + y], tbuf.at[4 * (2 * near + core) + y], z_send, z_recv.at[near], to)
 
     onward(0).start()
+    whole = remote(tbuf.at[pl.ds(16, 4)], tbuf.at[pl.ds(20, 4)], w_send, w_recv, partner)
+
+    @pl.when(core == 0)
+    def _():
+        whole.start()
 
     loads[2].wait()
     for rb, h in enumerate(permuted(res_in[...].reshape(64, 1024), perm_ref)):
@@ -275,8 +284,6 @@
     res_acc[...] = jnp.zeros_like(res_acc)
     for load in loads[4:]:
         load.wait()
-    for share in shares:
-        share.wait_recv()
     onward(1).start()
 
     def forward(near, d):
@@ -301,30 +308,31 @@
             ]
         return copies
 
-    def solve(slots):
+    def solve(places):
         u, w, factors = [], [], []
-        for owner, slot in enumerate(slots):
-            s = (core if owner == 0 else 1 - core) + 3 - slot
+        for owner, (entry, place) in enumerate(places):
+            s = (core if owner == 0 else 1 - core) + 3 - entry
             both = []
             for t in range(2):
-                wide = tbuf[pl.ds(4 * slot, 4), t].astype(F32).reshape(4, 2, 8, 512)
+                wide = tbuf[pl.ds(place, 4), t].astype(F32).reshape(4, 2, 8, 512)
                 both.append([wide[:, rb] for rb in range(2)])
             for p in range(2):
                 r, t, active = (spread(table[owner, s, 2 * e + p], 4)[None] for e in range(3))
                 u.append([jnp.where(r > 0.5, ubuf[owner, 1, rb], ubuf[owner, 0, rb]) for rb in range(2)])
                 w.append([jnp.where(t > 0.5, both[1][rb], both[0][rb]) for rb in range(2)])
                 factors.append([[active - active * e, active * e] for e in (r, t)])
+        fields = 2 * len(places)
         d = [
-            jnp.concatenate([(u[f][rb] * w[f][rb]).reshape(32, 512) for f in range(4)], axis=0)
+            jnp.concatenate([(u[f][rb] * w[f][rb]).reshape(32, 512) for f in range(fields)], axis=0)
             for rb in range(2)
         ]
         g = []
         for e in (d[0] + d[1], d[0] - d[1]):
             g += [e[:, :256] + e[:, 256:], e[:, :256] - e[:, 256:]]
-        rows = weight_ref[16]
+        rows = weight_ref[16] if fields == 4 else weight_ref[17, :128, :128]
         g = along_rows(plane(g, weight_ref, 0), rows)
         g = [
-            (m.reshape(4, 32, 256) * scale_ref[p][None]).reshape(128, 256)
+            (m.reshape(fields, 32, 256) * scale_ref[p][None]).reshape(fields * 32, 256)
             for p, m in enumerate(g)
         ]
         g = plane(along_rows(g, rows), weight_ref, 1)
@@ -335,14 +343,16 @@
         ):
             pot.append(jnp.concatenate([e + o, e - o], axis=1))
         for rb in range(2):
-            v = [pot[rb][f * 32 : (f + 1) * 32].reshape(4, 8, 512) for f in range(4)]
-            for owner in range(2):
-                f, f1 = 2 * owner, 2 * owner + 1
-                vw, vw1 = v[f] * w[f][rb], v[f1] * w[f1][rb]
-                vu, vu1 = v[f] * u[f][rb], v[f1] * u[f1][rb]
+            v = [pot[rb][f * 32 : (f + 1) * 32].reshape(4, 8, 512) for f in range(fields)]
+            theirs = [[], []]
+            for f in range(0, fields, 2):
+                vw, vw1 = v[f] * w[f][rb], v[f + 1] * w[f + 1][rb]
+                vu, vu1 = v[f] * u[f][rb], v[f + 1] * u[f + 1][rb]
                 for j in range(2):
-                    res_acc[owner, j, rb] += vw * factors[f][0][j] + vw1 * factors[f1][0][j]
-                    terms[owner, :, j, rb] = vu * factors[f][1][j] + vu1 * factors[f1][1][j]
+                    res_acc[f // 2, j, rb] += vw * factors[f][0][j] + vw1 * factors[f + 1][0][j]
+                    theirs[j].append(vu * factors[f][1][j] + vu1 * factors[f + 1][1][j])
+            for j in range(2):
+                terms[:, j, rb] = sum(theirs[j][1:], theirs[j][0])
 
     def one_row(tiles):
         top = jnp.max(peak(tiles), axis=0, keepdims=True)
@@ -376,12 +386,14 @@
         return [code[rb * 8 : (rb + 1) * 8] * scale for rb in range(2)]
 
     def homeward(e):
-        @pl.when(lax.rem(e, 2) == 0)
+        from_0 = jnp.logical_or(e == 0, e == 2)
+
+        @pl.when(from_0)
         def _():
             came(yget.at[e], y_recv.at[e])
             came(ygets.at[e, pl.ds(0, 4)], ys_recv.at[e])
 
-        @pl.when(lax.rem(e, 2) == 1)
+        @pl.when(jnp.logical_not(from_0))
         def _():
             came(yget.at[e, pl.ds(1, 3)], y_recv.at[e])
             came(ygets.at[e, pl.ds(1, 3)], ys_recv.at[e])
@@ -405,37 +417,49 @@
             copy.start()
 
     def step(i, carry):
-        @pl.when(i == 0)
+        @pl.when(jnp.logical_and(i == 0, core == 1))
+        def _():
+            whole.wait_recv()
+
+        @pl.when(i == 1)
         def _():
             for near in range(2):
                 came(tbuf.at[4 * (2 * near + core) + y], z_recv.at[near])
                 for d in (2, 1, 3):
                     forward(near, d).start()
-
-        came(tbuf.at[pl.ds(0, 3)], f_recv.at[i])
-        slot = 2 * i + core
-        apart = (1 - core) * (1 - i)
-        solve((slot, slot + 4 * apart))
-
-        @pl.when(apart == 0)
-        def _():
-            terms[0] += terms[1]
-
-        def send(k, inner):
-            over_y(slot + 4 * k, terms[k])
-            return inner
-
-        lax.fori_loop(0, 1 + apart, send, 0)
+            for share in shares:
+                share.wait_recv()
+
+        @pl.when(i > 0)
+        def _():
+            came(tbuf.at[pl.ds(0, 3)], f_recv.at[i - 1])
+
+        alone = i + core == 1
+
+        @pl.when(alone)
+        def _():
+            solve(((4 * core, 20 * core),))
+
+        slot = 2 * (i - 1) + core
+
+        @pl.when(i + core >= 2)
+        def _():
+            solve(((slot, 4 * slot), (slot, 4 * slot)))
+
+        @pl.when(i + core >= 1)
+        def _():
+            one = (1 - (i + core) // 2) * (i + core)
+            over_y(one * 4 * core + (1 - one) * slot, terms[...])
+
         return carry
 
-    lax.fori_loop(0, 2, step, 0)
+    lax.fori_loop(0, 3, step, 0)
 
     back = remote(res_acc.at[1], res_got, r_send, r_recv, partner)
     back.start()
 
     def send_home(j, carry):
-        even = (j + 3) // 5
-        homeward((1 - even) * (2 * j + 1) + even * lax.rem(4 * j + 4, 6))
+        homeward(lax.rem(4 + 2 * j, 5))
         return carry
 
     @pl.when(core == 1)
@@ -477,13 +501,14 @@
 
     @pl.when(core == 0)
     def _():
-        left(ycode.at[pl.ds(0, 12)], y_send)
-        left(ysent.at[pl.ds(0, 12)], ys_send)
+        whole.wait_send()
+        left(ycode.at[pl.ds(0, 8)], y_send)
+        left(ysent.at[pl.ds(0, 8)], ys_send)
 
     @pl.when(core == 1)
     def _():
-        left(ycode.at[pl.ds(0, 6)], y_send)
-        left(ysent.at[pl.ds(0, 6)], ys_send)
+        left(ycode.at[pl.ds(0, 9)], y_send)
+        left(ysent.at[pl.ds(0, 9)], ys_send)
         left(hcode, h_send)
         left(ysent.at[pl.ds(0, 10)], hs_send)
 
@@ -514,15 +539,15 @@
             pltpu.VMEM((2, 32, 1024), BF16),
             pltpu.SMEM((1, 3, 2, 4), jnp.int32),
             pltpu.VMEM((4, 256, 256), BF16),
-            pltpu.VMEM((17, 256, 256), BF16),
+            pltpu.VMEM((18, 256, 256), BF16),
             pltpu.VMEM((4, 32, 256), F32),
             dma((6,)),
-            pltpu.VMEM((20, 2, 16, 512), BF16),
+            pltpu.VMEM((24, 2, 16, 512), BF16),
             pltpu.VMEM((2, 2, 2, 4, 8, 512), F32),
             pltpu.VMEM((2, 4, 6, 8, 128), F32),
             pltpu.VMEM((2, 2, 2, 4, 8, 512), F32),
             pltpu.VMEM((2, 2, 4, 8, 512), F32),
-            pltpu.VMEM((2, 4, 2, 2, 8, 512), F32),
+            pltpu.VMEM((4, 2, 2, 8, 512), F32),
             pltpu.VMEM((20, 2, 16, 512), I16),
             pltpu.VMEM((8, 128), F32),
             pltpu.VMEM((16, 128), F32),
@@ -537,6 +562,8 @@
             dma((2,)),
             dma,
             dma((2,)),
+            dma,
+            dma,
             dma,
             dma,
             dma,

time: 29.7 us -> 29.1 us (0.980)
  the two profiles are of different devices: /device:TPU:1 before, /device:TPU:8 now
where the time goes in v8:
time: 29.1 us; the launch traced here: 29 us
  Pallas kernels  28.3 us (97%)
  between operations  0.64 us (2%)
    pallas_call x1, Pallas kernels, local(): pl.pallas_call(kernel, out_shape=(pltpu.VMEM((2, 32, 1024), F32), pltpu.V...  27.6 us
    pallas_call x1, Pallas kernels, local(): pl.pallas_call(store, out_shape=(jax.ShapeDtypeStruct((2, 32, 1024), F32)...  0.72 us

profile of v8, /device:TPU:8, one launch (start us, length us, event | category | flops | bytes accessed | tf_op | source)
XLA Modules:
  0.0 29.0 jit_solution(17364783690659655017)
XLA Ops:
  0.6 27.6 %shard_map.77 = (f32[2,32,1024]{2,1,0:T(8,128)S(1)}, f32[2,4,1024]{2,1,0:T(4,128)S(1)}) custom-call(bf16[2,32,1024]{2,1,0:T(8,128)(2,1)} %res_hbm.1, bf16[2,32,1024]{2,1,0:T(8,128)(2,1)} %trav_hbm.1, s32[1,3,2,4]{3,2,1,0:T(2,128)} %bitcast.1, bf16[4,256,256]{2,1,0:T(8,128)(2,1)} %constant.6.clone.perm_hbm, bf16[18,256,256]{2,1,0:T(8,128)(2,1)} %constant.7.clone.weight_hbm, ...), custom_call_target="tpu_custom_call" | custom-call | tf_op jit(solution)/shard_map/pallas_call | solution.py:532
  28.3 0.7 %shard_map.78 = (f32[2,32,1024]{2,1,0:T(8,128)}, f32[2,4,1024]{2,1,0:T(4,128)}) custom-call(f32[2,32,1024]{2,1,0:T(8,128)S(1)} %get-tuple-element.4.res_ref, f32[2,4,1024]{2,1,0:T(4,128)S(1)} %get-tuple-element.5.trav_ref), custom_call_target="tpu_custom_call" | custom-call | tf_op jit(solution)/shard_map/pallas_call | solution.py:586

commit v9 on v8

--- a/solution.py
+++ b/solution.py
@@ -171,8 +171,6 @@
     z_recv,
     f_send,
     f_recv,
-    w_send,
-    w_recv,
     u_send,
     u_recv,
     p_send,
@@ -234,7 +232,6 @@
     def arrive(to):
         pl.semaphore_signal(barrier, inc=1, device_id=to, device_id_type=MESH)
 
-    arrive((around(blk - 4), across_z))
     arrive((around(blk - 2), grp))
     for d in range(1, 4):
         arrive((blk, y_peer(d) * 2 + lo))
@@ -243,6 +240,8 @@
 
     @pl.when(core == 1)
     def _():
+        for c in range(2):
+            arrive((around(first - 4 + c), across_z))
         for d in range(1, 4):
             arrive((first, y_peer(d) * 2 + lo))
 
@@ -256,15 +255,11 @@
     pl.semaphore_wait(barrier, 7 + 3 * (1 - core))
 
     def onward(near):
-        to = (around(blk + 2), grp) if near else (around(blk + 4), across_z)
-        return remote(tbuf.at[16 + y], tbuf.at[4 * (2 * near + core) + y], z_send, z_recv.at[near], to)
+        to = (around(blk + 2), grp) if near else (around(first + 5), across_z)
+        slot = 2 * near + core
+        return remote(tbuf.at[16 + y], tbuf.at[4 * slot + y], z_send, z_recv.at[slot], to)
 
     onward(0).start()
-    whole = remote(tbuf.at[pl.ds(16, 4)], tbuf.at[pl.ds(20, 4)], w_send, w_recv, partner)
-
-    @pl.when(core == 0)
-    def _():
-        whole.start()
 
     loads[2].wait()
     for rb, h in enumerate(permuted(res_in[...].reshape(64, 1024), perm_ref)):
@@ -286,9 +281,11 @@
         load.wait()
     onward(1).start()
 
-    def forward(near, d):
-        at = 4 * (2 * near + core) + y
-        return remote(tbuf.at[at], tbuf.at[at], f_send, f_recv.at[near], (blk, y_peer(d) * 2 + lo))
+    def relay(slot):
+        at = 4 * slot + y
+        came(tbuf.at[at], z_recv.at[slot])
+        for d in (2, 1, 3):
+            remote(tbuf.at[at], tbuf.at[at], f_send, f_recv.at[slot], (blk, y_peer(d) * 2 + lo)).start()
 
     def y_copies(e, d):
         to = (first + 1, y_peer(d) * 2 + lo)
@@ -310,7 +307,7 @@
 
     def solve(places):
         u, w, factors = [], [], []
-        for owner, (entry, place) in enumerate(places):
+        for owner, entry, place in places:
             s = (core if owner == 0 else 1 - core) + 3 - entry
             both = []
             for t in range(2):
@@ -349,7 +346,7 @@
                 vw, vw1 = v[f] * w[f][rb], v[f + 1] * w[f + 1][rb]
                 vu, vu1 = v[f] * u[f][rb], v[f + 1] * u[f + 1][rb]
                 for j in range(2):
-                    res_acc[f // 2, j, rb] += vw * factors[f][0][j] + vw1 * factors[f + 1][0][j]
+                    res_acc[places[f // 2][0], j, rb] += vw * factors[f][0][j] + vw1 * factors[f + 1][0][j]
                     theirs[j].append(vu * factors[f][1][j] + vu1 * factors[f + 1][1][j])
             for j in range(2):
                 terms[:, j, rb] = sum(theirs[j][1:], theirs[j][0])
@@ -386,7 +383,7 @@
         return [code[rb * 8 : (rb + 1) * 8] * scale for rb in range(2)]
 
     def homeward(e):
-        from_0 = jnp.logical_or(e == 0, e == 2)
+        from_0 = jnp.logical_or(e == 4, e == 2)
 
         @pl.when(from_0)
         def _():
@@ -419,37 +416,41 @@
     def step(i, carry):
         @pl.when(jnp.logical_and(i == 0, core == 1))
         def _():
-            whole.wait_recv()
-
-        @pl.when(i == 1)
-        def _():
-            for near in range(2):
-                came(tbuf.at[4 * (2 * near + core) + y], z_recv.at[near])
-                for d in (2, 1, 3):
-                    forward(near, d).start()
+            for slot in (1, 3, 0):
+                relay(slot)
+
+        @pl.when(jnp.logical_and(i == 1, core == 0))
+        def _():
+            relay(2)
+
+        @pl.when(i == 0)
+        def _():
             for share in shares:
                 share.wait_recv()
 
-        @pl.when(i > 0)
-        def _():
-            came(tbuf.at[pl.ds(0, 3)], f_recv.at[i - 1])
-
-        alone = i + core == 1
+        entry = 2 * i + core
+        alone = i == 2 * core
+        one = 1 - ((i - 2 * core) * (i - 2 * core) + 3) // 4
+        single = 4 * (1 - core)
+
+        @pl.when(jnp.logical_and(alone, core == 1))
+        def _():
+            came(tbuf.at[pl.ds(0, 3)], f_recv.at[0])
 
         @pl.when(alone)
         def _():
-            solve(((4 * core, 20 * core),))
-
-        slot = 2 * (i - 1) + core
-
-        @pl.when(i + core >= 2)
-        def _():
-            solve(((slot, 4 * slot), (slot, 4 * slot)))
-
-        @pl.when(i + core >= 1)
-        def _():
-            one = (1 - (i + core) // 2) * (i + core)
-            over_y(one * 4 * core + (1 - one) * slot, terms[...])
+            solve(((1, single, 4 * single),))
+
+        full = jnp.logical_or(i == 1, jnp.logical_and(i == 0, core == 1))
+
+        @pl.when(full)
+        def _():
+            came(tbuf.at[pl.ds(0, 3)], f_recv.at[entry])
+            solve(((0, entry, 4 * entry), (1, entry, 4 * entry)))
+
+        @pl.when(jnp.logical_or(full, alone))
+        def _():
+            over_y(one * single + (1 - one) * entry, terms[...])
 
         return carry
 
@@ -494,19 +495,19 @@
     trav_out[...] = restored([total[rb] for rb in range(2)], perm_ref).reshape(2, 4, 1024)
 
     left(tbuf.at[pl.ds(0, 2)], z_send)
-    left(tbuf.at[pl.ds(0, 6)], f_send)
     for share in shares:
         share.wait_send()
     back.wait_send()
 
     @pl.when(core == 0)
     def _():
-        whole.wait_send()
+        left(tbuf.at[pl.ds(0, 3)], f_send)
         left(ycode.at[pl.ds(0, 8)], y_send)
         left(ysent.at[pl.ds(0, 8)], ys_send)
 
     @pl.when(core == 1)
     def _():
+        left(tbuf.at[pl.ds(0, 9)], f_send)
         left(ycode.at[pl.ds(0, 9)], y_send)
         left(ysent.at[pl.ds(0, 9)], ys_send)
         left(hcode, h_send)
@@ -542,7 +543,7 @@
             pltpu.VMEM((18, 256, 256), BF16),
             pltpu.VMEM((4, 32, 256), F32),
             dma((6,)),
-            pltpu.VMEM((24, 2, 16, 512), BF16),
+            pltpu.VMEM((20, 2, 16, 512), BF16),
             pltpu.VMEM((2, 2, 2, 4, 8, 512), F32),
             pltpu.VMEM((2, 4, 6, 8, 128), F32),
             pltpu.VMEM((2, 2, 2, 4, 8, 512), F32),
@@ -559,11 +560,9 @@
             pltpu.VMEM((8, 128), F32),
             pltpu.VMEM((2, 8, 512), F32),
             dma,
-            dma((2,)),
-            dma,
-            dma((2,)),
-            dma,
-            dma,
+            dma((4,)),
+            dma,
+            dma((4,)),
             dma,
             dma,
             dma,

time: 29.1 us -> 28.6 us (0.983)
  the two profiles are of different devices: /device:TPU:8 before, /device:TPU:1 now
where the time goes in v9:
time: 28.6 us; the launch traced here: 28.5 us
  Pallas kernels  27.9 us (98%)
  between operations  0.64 us (2%)
    pallas_call x1, Pallas kernels, local(): pl.pallas_call(kernel, out_shape=(pltpu.VMEM((2, 32, 1024), F32), pltpu.V...  27.1 us
    pallas_call x1, Pallas kernels, local(): pl.pallas_call(store, out_shape=(jax.ShapeDtypeStruct((2, 32, 1024), F32)...  0.72 us

profile of v9, /device:TPU:1, one launch (start us, length us, event | category | flops | bytes accessed | tf_op | source)
XLA Modules:
  0.0 28.5 jit_solution(4930852713905168517)
XLA Ops:
  0.6 27.1 %shard_map.77 = (f32[2,32,1024]{2,1,0:T(8,128)S(1)}, f32[2,4,1024]{2,1,0:T(4,128)S(1)}) custom-call(bf16[2,32,1024]{2,1,0:T(8,128)(2,1)} %res_hbm.1, bf16[2,32,1024]{2,1,0:T(8,128)(2,1)} %trav_hbm.1, s32[1,3,2,4]{3,2,1,0:T(2,128)} %bitcast.1, bf16[4,256,256]{2,1,0:T(8,128)(2,1)} %constant.6.clone.perm_hbm, bf16[18,256,256]{2,1,0:T(8,128)(2,1)} %constant.7.clone.weight_hbm, ...), custom_call_target="tpu_custom_call" | custom-call | tf_op jit(solution)/shard_map/pallas_call | solution.py:533
  27.8 0.7 %shard_map.78 = (f32[2,32,1024]{2,1,0:T(8,128)}, f32[2,4,1024]{2,1,0:T(4,128)}) custom-call(f32[2,32,1024]{2,1,0:T(8,128)S(1)} %get-tuple-element.4.res_ref, f32[2,4,1024]{2,1,0:T(4,128)S(1)} %get-tuple-element.5.trav_ref), custom_call_target="tpu_custom_call" | custom-call | tf_op jit(solution)/shard_map/pallas_call | solution.py:585

commit v10 on v9

--- a/solution.py
+++ b/solution.py
@@ -233,17 +233,15 @@
         pl.semaphore_signal(barrier, inc=1, device_id=to, device_id_type=MESH)
 
     arrive((around(blk - 2), grp))
+    arrive((first, across_z))
     for d in range(1, 4):
-        arrive((blk, y_peer(d) * 2 + lo))
-    arrive((blk, across_z))
-    arrive(partner)
+        arrive((first, y_peer(d) * 2 + lo))
 
     @pl.when(core == 1)
     def _():
         for c in range(2):
             arrive((around(first - 4 + c), across_z))
-        for d in range(1, 4):
-            arrive((first, y_peer(d) * 2 + lo))
+        arrive(partner)
 
     loads[0].wait()
     loads[1].wait()
@@ -252,7 +250,7 @@
         for t in range(2):
             tbuf[16 + q, t] = jnp.concatenate([own[0][t, q], own[1][t, q]], axis=0).astype(BF16)
 
-    pl.semaphore_wait(barrier, 7 + 3 * (1 - core))
+    pl.semaphore_wait(barrier, 2 + 9 * (1 - core))
 
     def onward(near):
         to = (around(blk + 2), grp) if near else (around(first + 5), across_z)
@@ -274,8 +272,12 @@
         remote(ubuf.at[0], ubuf.at[1], u_send, u_recv, partner),
         remote(table.at[0], table.at[1], p_send, p_recv, partner),
     ]
-    for share in shares:
-        share.start()
+
+    @pl.when(core == 0)
+    def _():
+        for share in shares:
+            share.start()
+
     res_acc[...] = jnp.zeros_like(res_acc)
     for load in loads[4:]:
         load.wait()
@@ -416,6 +418,10 @@
     def step(i, carry):
         @pl.when(jnp.logical_and(i == 0, core == 1))
         def _():
+            for share in shares:
+                share.wait_recv()
+            for share in shares:
+                share.start()
             for slot in (1, 3, 0):
                 relay(slot)
 
@@ -423,7 +429,7 @@
         def _():
             relay(2)
 
-        @pl.when(i == 0)
+        @pl.when(jnp.logical_and(i == 0, core == 0))
         def _():
             for share in shares:
                 share.wait_recv()

time: 28.6 us -> 28.7 us (level); the launches traced: 28.5 us -> 28.3 us
  no operation moved by 1% of the time
where the time goes in v10:
time: 28.7 us; the launch traced here: 28.3 us
  Pallas kernels  27.7 us (97%)
  between operations  0.64 us (2%)
    pallas_call x1, Pallas kernels, local(): pl.pallas_call(kernel, out_shape=(pltpu.VMEM((2, 32, 1024), F32), pltpu.V...  26.9 us
    pallas_call x1, Pallas kernels, local(): pl.pallas_call(store, out_shape=(jax.ShapeDtypeStruct((2, 32, 1024), F32)...  0.72 us

profile of v10, /device:TPU:1, one launch (start us, length us, event | category | flops | bytes accessed | tf_op | source)
XLA Modules:
  0.0 28.3 jit_solution(13184878770700387101)
XLA Ops:
  0.6 26.9 %shard_map.77 = (f32[2,32,1024]{2,1,0:T(8,128)S(1)}, f32[2,4,1024]{2,1,0:T(4,128)S(1)}) custom-call(bf16[2,32,1024]{2,1,0:T(8,128)(2,1)} %res_hbm.1, bf16[2,32,1024]{2,1,0:T(8,128)(2,1)} %trav_hbm.1, s32[1,3,2,4]{3,2,1,0:T(2,128)} %bitcast.1, bf16[4,256,256]{2,1,0:T(8,128)(2,1)} %constant.6.clone.perm_hbm, bf16[18,256,256]{2,1,0:T(8,128)(2,1)} %constant.7.clone.weight_hbm, ...), custom_call_target="tpu_custom_call" | custom-call | tf_op jit(solution)/shard_map/pallas_call | solution.py:539
  27.6 0.7 %shard_map.78 = (f32[2,32,1024]{2,1,0:T(8,128)}, f32[2,4,1024]{2,1,0:T(4,128)}) custom-call(f32[2,32,1024]{2,1,0:T(8,128)S(1)} %get-tuple-element.4.res_ref, f32[2,4,1024]{2,1,0:T(4,128)S(1)} %get-tuple-element.5.trav_ref), custom_call_target="tpu_custom_call" | custom-call | tf_op jit(solution)/shard_map/pallas_call | solution.py:591

commit v11 on v9

--- a/solution.py
+++ b/solution.py
@@ -156,7 +156,6 @@
     table,
     res_acc,
     res_got,
-    terms,
     ycode,
     yscale,
     ysent,
@@ -339,6 +338,7 @@
             (g[0] - g[2], g[1] - g[3]),
         ):
             pot.append(jnp.concatenate([e + o, e - o], axis=1))
+        terms = [[], []]
         for rb in range(2):
             v = [pot[rb][f * 32 : (f + 1) * 32].reshape(4, 8, 512) for f in range(fields)]
             theirs = [[], []]
@@ -349,7 +349,8 @@
                     res_acc[places[f // 2][0], j, rb] += vw * factors[f][0][j] + vw1 * factors[f + 1][0][j]
                     theirs[j].append(vu * factors[f][1][j] + vu1 * factors[f + 1][1][j])
             for j in range(2):
-                terms[:, j, rb] = sum(theirs[j][1:], theirs[j][0])
+                terms[j].append(sum(theirs[j][1:], theirs[j][0]))
+        return terms
 
     def one_row(tiles):
         top = jnp.max(peak(tiles), axis=0, keepdims=True)
@@ -357,12 +358,12 @@
 
     def over_y(e, value):
         parts = [(q, t, rb) for q in range(4) for t in range(2) for rb in range(2)]
-        top, wide = one_row([x for at in parts for x in lane_tiles(value[at])])
+        top, wide = one_row([x for at in parts for x in lane_tiles(value[at[1]][at[2]][at[0]])])
         yscale[pl.ds(e, 1)] = top * (1.0 / TOP)
         wide = spread(wide, 4)
         for q in range(4):
             for t in range(2):
-                ycode[4 * e + q, t] = jnp.concatenate([coded(value[q, t, rb], wide) for rb in range(2)], axis=0).astype(I16)
+                ycode[4 * e + q, t] = jnp.concatenate([coded(value[t][rb][q], wide) for rb in range(2)], axis=0).astype(I16)
         for d in (2, 1, 3):
             for copy in y_copies(e, d):
                 copy.start()
@@ -430,7 +431,6 @@
 
         entry = 2 * i + core
         alone = i == 2 * core
-        one = 1 - ((i - 2 * core) * (i - 2 * core) + 3) // 4
         single = 4 * (1 - core)
 
         @pl.when(jnp.logical_and(alone, core == 1))
@@ -439,18 +439,14 @@
 
         @pl.when(alone)
         def _():
-            solve(((1, single, 4 * single),))
+            over_y(single, solve(((1, single, 4 * single),)))
 
         full = jnp.logical_or(i == 1, jnp.logical_and(i == 0, core == 1))
 
         @pl.when(full)
         def _():
             came(tbuf.at[pl.ds(0, 3)], f_recv.at[entry])
-            solve(((0, entry, 4 * entry), (1, entry, 4 * entry)))
-
-        @pl.when(jnp.logical_or(full, alone))
-        def _():
-            over_y(one * single + (1 - one) * entry, terms[...])
+            over_y(entry, solve(((0, entry, 4 * entry), (1, entry, 4 * entry))))
 
         return carry
 
@@ -548,7 +544,6 @@
             pltpu.VMEM((2, 4, 6, 8, 128), F32),
             pltpu.VMEM((2, 2, 2, 4, 8, 512), F32),
             pltpu.VMEM((2, 2, 4, 8, 512), F32),
-            pltpu.VMEM((4, 2, 2, 8, 512), F32),
             pltpu.VMEM((20, 2, 16, 512), I16),
             pltpu.VMEM((8, 128), F32),
             pltpu.VMEM((16, 128), F32),

time: 28.6 us -> 29 us (1.014)
  Pallas kernels: 27.9 us -> 28.3 us
    pallas_call x1, Pallas kernels: 27.1 us -> 27.6 us  [local(): pl.pallas_call(kernel, out_shape=(pltpu.VMEM((2, 32, 1024), F32), pltpu.V...]
where the time goes in v11:
time: 29 us; the launch traced here: 28.9 us
  Pallas kernels  28.3 us (98%)
  between operations  0.64 us (2%)
    pallas_call x1, Pallas kernels, local(): pl.pallas_call(kernel, out_shape=(pltpu.VMEM((2, 32, 1024), F32), pltpu.V...  27.6 us
    pallas_call x1, Pallas kernels, local(): pl.pallas_call(store, out_shape=(jax.ShapeDtypeStruct((2, 32, 1024), F32)...  0.72 us

profile of v11, /device:TPU:1, one launch (start us, length us, event | category | flops | bytes accessed | tf_op | source)
XLA Modules:
  0.0 28.9 jit_solution(11096182821288970530)
XLA Ops:
  0.6 27.6 %shard_map.77 = (f32[2,32,1024]{2,1,0:T(8,128)S(1)}, f32[2,4,1024]{2,1,0:T(4,128)S(1)}) custom-call(bf16[2,32,1024]{2,1,0:T(8,128)(2,1)} %res_hbm.1, bf16[2,32,1024]{2,1,0:T(8,128)(2,1)} %trav_hbm.1, s32[1,3,2,4]{3,2,1,0:T(2,128)} %bitcast.1, bf16[4,256,256]{2,1,0:T(8,128)(2,1)} %constant.6.clone.perm_hbm, bf16[18,256,256]{2,1,0:T(8,128)(2,1)} %constant.7.clone.weight_hbm, ...), custom_call_target="tpu_custom_call" | custom-call | tf_op jit(solution)/shard_map/pallas_call | solution.py:529
  28.2 0.7 %shard_map.78 = (f32[2,32,1024]{2,1,0:T(8,128)}, f32[2,4,1024]{2,1,0:T(4,128)}) custom-call(f32[2,32,1024]{2,1,0:T(8,128)S(1)} %get-tuple-element.4.res_ref, f32[2,4,1024]{2,1,0:T(4,128)S(1)} %get-tuple-element.5.trav_ref), custom_call_target="tpu_custom_call" | custom-call | tf_op jit(solution)/shard_map/pallas_call | solution.py:580

commit v12 on v9

--- a/solution.py
+++ b/solution.py
@@ -279,7 +279,10 @@
     res_acc[...] = jnp.zeros_like(res_acc)
     for load in loads[4:]:
         load.wait()
-    onward(1).start()
+
+    @pl.when(core == 1)
+    def _():
+        onward(1).start()
 
     def relay(slot):
         at = 4 * slot + y
@@ -428,6 +431,10 @@
             for share in shares:
                 share.wait_recv()
 
+        @pl.when(jnp.logical_and(i == 0, core == 0))
+        def _():
+            onward(1).start()
+
         entry = 2 * i + core
         alone = i == 2 * core
         one = 1 - ((i - 2 * core) * (i - 2 * core) + 3) // 4

time: 28.6 us -> 28.7 us (level)
  no operation moved by 1% of the time
where the time goes in v12:
time: 28.7 us; the launch traced here: 28.6 us
  Pallas kernels  28 us (98%)
  between operations  0.64 us (2%)
    pallas_call x1, Pallas kernels, local(): pl.pallas_call(kernel, out_shape=(pltpu.VMEM((2, 32, 1024), F32), pltpu.V...  27.3 us
    pallas_call x1, Pallas kernels, local(): pl.pallas_call(store, out_shape=(jax.ShapeDtypeStruct((2, 32, 1024), F32)...  0.72 us

profile of v12, /device:TPU:1, one launch (start us, length us, event | category | flops | bytes accessed | tf_op | source)
XLA Modules:
  0.0 28.6 jit_solution(533129338635507770)
XLA Ops:
  0.6 27.3 %shard_map.77 = (f32[2,32,1024]{2,1,0:T(8,128)S(1)}, f32[2,4,1024]{2,1,0:T(4,128)S(1)}) custom-call(bf16[2,32,1024]{2,1,0:T(8,128)(2,1)} %res_hbm.1, bf16[2,32,1024]{2,1,0:T(8,128)(2,1)} %trav_hbm.1, s32[1,3,2,4]{3,2,1,0:T(2,128)} %bitcast.1, bf16[4,256,256]{2,1,0:T(8,128)(2,1)} %constant.6.clone.perm_hbm, bf16[18,256,256]{2,1,0:T(8,128)(2,1)} %constant.7.clone.weight_hbm, ...), custom_call_target="tpu_custom_call" | custom-call | tf_op jit(solution)/shard_map/pallas_call | solution.py:540
  27.9 0.7 %shard_map.78 = (f32[2,32,1024]{2,1,0:T(8,128)}, f32[2,4,1024]{2,1,0:T(4,128)}) custom-call(f32[2,32,1024]{2,1,0:T(8,128)S(1)} %get-tuple-element.4.res_ref, f32[2,4,1024]{2,1,0:T(4,128)S(1)} %get-tuple-element.5.trav_ref), custom_call_target="tpu_custom_call" | custom-call | tf_op jit(solution)/shard_map/pallas_call | solution.py:592
